TPU v7x, 32 devices: a whole 2x2x4 slice. The times are simulated.
32 devices in a mesh: blk: 16 (over z, y, x), grp: 2 (over core).
Axes of the slice: x: 2, y: 2, z: 4, core: 2. Of those that a mesh axis runs over, the one named last changes fastest.
Arguments:
- sky_maps: float32 [4, 128, 4096], P(None, ('blk', 'grp')), may hold values from -6 to 6
- legendre: bfloat16 [128, 512, 2048], P(('blk', 'grp')), may hold values from -0.5 to 0.5
- owner_table: int32 [512], replicated, may hold values from 0 to 511, each once
Outputs:
- harmonics: float32 [512, 4, 2, 2048], P(('blk', 'grp'))
- spectra: float32 [10, 2048], P(None, ('blk', 'grp'))
Inputs may be any that keep to these rules, and one draw needn't show every extreme that they name: `owner_table`: a permutation of the orders 0 to 511.
All inputs are finite; a program needn't handle non-finite values.
Results may differ from a plain program's by a relative error of at most 0.0034.
Values may be sent and summed in bfloat16 or wider, within the bound.
A program may use at most 128 MiB of HBM per device.

v0:
```python
import functools
import math

import jax
import jax.numpy as jnp
import numpy as np
from jax import lax
from jax.experimental import pallas as pl
from jax.experimental.pallas import tpu as pltpu
from jax.sharding import PartitionSpec as P

AXES = ("blk", "grp")
MIB = 1024 * 1024
MESH = pl.DeviceIdType.MESH
BF16 = jnp.bfloat16
F32 = jnp.float32
GROUP = 16
FIRST = (1, 2)
EARLY = 3
WIDTH = 256


def plan_of(bits):
    later = [[EARLY] + [b for b in range(1, bits) if b not in (first, EARLY)] for first in FIRST]
    return later


def flip(me, bits):
    out = me
    for b in bits:
        out = out + (1 - 2 * ((me // (1 << b)) % 2)) * (1 << b)
    return out


def split_bf16(values):
    high = values.astype(BF16)
    low = (values - high.astype(F32)).astype(BF16)
    return high, low


def dot(left, right):
    return jnp.dot(left, right, preferred_element_type=F32)


def dot_t(left, right):
    return lax.dot_general(left, right, (((1,), (1,)), ((), ())), preferred_element_type=F32)


def fourier_tables(pixels, order_count, width):
    coarse = pixels // width
    k1, m1 = np.meshgrid(np.arange(coarse), np.arange(coarse), indexing="ij")
    angle = 2.0 * math.pi * ((k1 * m1) % coarse) / coarse
    first = np.concatenate([np.cos(angle.T), -np.sin(angle.T)], axis=0)
    k2 = np.arange(width)[:, None]
    m = np.arange(order_count)[None, :]
    angle = 2.0 * math.pi * ((k2 * m) % pixels) / pixels
    cosine, sine = np.cos(angle) / math.sqrt(pixels), np.sin(angle) / math.sqrt(pixels)
    second = np.block([[cosine, -sine], [sine, cosine]]).astype(np.float32)
    high = second.astype(jnp.bfloat16)
    low = (second - high.astype(np.float32)).astype(jnp.bfloat16)
    return first.astype(np.float32), high, low


def kernel(
    cfg, owner_smem, owner_ref, sky_hbm, first_hbm, high_hbm, low_hbm, leg_hbm, harm_ref, spec_ref,
    leg_v, sky_v, first_v, high_v, low_v, hot_v, lhs_v, own0, send0, recv0, coef_own, coef_send, coef_recv,
    acc_v, halves, pow_v, pow_recv, pow_mine, pow_pair, load_sem, sky_sem, table_sem,
    sems0, coef_sems, half_sems, pow_sems, pair_sems,
):
    maps, cycles, orders, ells, devices, grp, width = cfg
    bits = devices.bit_length() - 1
    later = plan_of(bits)
    steps = bits - 2
    chunks = ells // width
    channels = 2 * maps
    own = orders // devices
    per_type = own // 2
    block = orders // 8
    rows0 = block * channels
    me = lax.axis_index("blk") * grp + lax.axis_index("grp")
    tile = 128
    tiles = ells // tile
    sharers = tile * devices // ells
    pairs = maps * (maps + 1) // 2

    def at(index):
        return (index // grp, index % grp)

    def bit(b):
        return (me // (1 << b)) % 2

    gather = [[None, flip(me, [0]), flip(me, [FIRST[ty]]), flip(me, [FIRST[ty], 0])] for ty in range(2)]
    near = sorted({(0,)} | {(f,) for f in FIRST} | {(0, f) for f in FIRST} | {(b,) for b in range(1, bits)})

    barrier = pltpu.get_barrier_semaphore()
    for masks in near:
        pl.semaphore_signal(barrier, inc=1, device_id=at(flip(me, masks)), device_id_type=MESH)

    def load(t):
        lanes = pl.ds(pl.multiple_of(t * width, width), width)
        return pltpu.make_async_copy(leg_hbm.at[:, :, lanes], leg_v.at[t], load_sem.at[t])

    def load_start(t, carry):
        load(t).start()
        return carry

    lax.fori_loop(0, chunks, load_start, 0)
    coarse = sky_v.shape[2]

    def sky_load(k):
        lanes = pl.ds(pl.multiple_of(k * tile, tile), tile)
        return pltpu.make_async_copy(sky_hbm.at[:, :, lanes], sky_v.at[:, :, k, :], sky_sem.at[k])

    def sky_start(k, carry):
        sky_load(k).start()
        return carry

    lax.fori_loop(0, coarse, sky_start, 0)
    tables = [
        pltpu.make_async_copy(src, dst, table_sem.at[i])
        for i, (src, dst) in enumerate(((first_hbm, first_v), (high_hbm, high_v), (low_hbm, low_v)))
    ]
    for table in tables:
        table.start()

    j = lax.broadcasted_iota(jnp.int32, (orders, tile), 0)
    part = j // (orders // 2)
    rest = j % block
    slot = part * per_type + rest % per_type

    def place(b, differs):
        mine = bit(b)
        return (mine + differs - 2 * mine * differs) * ((1 << b) * own)

    slot = slot + place(0, (j // block) % 2)
    for ty in range(2):
        terms = place(FIRST[ty], (j // (2 * block)) % 2)
        for s, b in enumerate(later[ty]):
            terms = terms + place(b, (rest // (block >> (s + 1))) % 2)
        slot = slot + jnp.where(part == ty, terms, 0)
    lane = lax.broadcasted_iota(jnp.int32, (orders, tile), 1)
    pick = jnp.concatenate(
        [jnp.where(slot == lane + c * tile, 1.0, 0.0).astype(BF16) for c in range(orders // tile)], axis=1
    )
    table = jnp.where(lax.broadcasted_iota(jnp.int32, (orders, orders), 0) == owner_ref[...], 1.0, 0.0).astype(BF16)
    hot_v[...] = dot_t(pick, table).astype(BF16)

    def gather_copy(ty, t, p):
        return pltpu.make_async_remote_copy(
            src_ref=send0.at[ty, t, p - 1],
            dst_ref=recv0.at[ty, t, p - 1],
            send_sem=sems0.at[0, ty, t, p - 1],
            recv_sem=sems0.at[1, ty, t, p - 1],
            device_id=at(gather[ty][p]),
            device_id_type=MESH,
        )

    def coef_copy(ty, p):
        return pltpu.make_async_remote_copy(
            src_ref=coef_send.at[ty, p - 1],
            dst_ref=coef_recv.at[ty, p - 1],
            send_sem=coef_sems.at[0, ty, p - 1],
            recv_sem=coef_sems.at[1, ty, p - 1],
            device_id=at(gather[ty][p]),
            device_id_type=MESH,
        )

    def half_copy(s, ty, t):
        return pltpu.make_async_remote_copy(
            src_ref=halves[2 * s].at[ty, t],
            dst_ref=halves[2 * s + 1].at[ty, t],
            send_sem=half_sems.at[0, s, ty, t],
            recv_sem=half_sems.at[1, s, ty, t],
            device_id=at(flip(me, [later[ty][s]])),
            device_id_type=MESH,
        )

    def permute(t):
        load(t).wait()
        for r in range(cycles):
            values = leg_v[t, r]
            for ty in range(2):
                picked = dot(hot_v[ty * 4 * block : (ty + 1) * 4 * block, :], values).astype(BF16)
                own0[ty, t, r] = picked[:block]
                for p in range(1, 4):
                    send0[ty, t, p - 1, r] = picked[p * block : (p + 1) * block]
        for p in (2, 3, 1):
            for ty in range(2):
                gather_copy(ty, t, p).start()

    pl.semaphore_wait(barrier, len(near))
    permute(0)

    def sky_wait(k, carry):
        sky_load(k).wait()
        return carry

    lax.fori_loop(0, coarse, sky_wait, 0)
    for table in tables:
        table.wait()
    count = maps * cycles
    columns = 2 * orders
    stages = []
    first = first_v[...]
    for b in range(count):
        stage = jnp.dot(
            first, sky_v[b // cycles, b % cycles], precision=lax.Precision.HIGHEST, preferred_element_type=F32
        )
        stages.append(jnp.concatenate([stage[:coarse], stage[coarse:]], axis=1))
    left_high, left_low = split_bf16(jnp.concatenate(stages, axis=0))
    spectral = []
    span = orders // 2
    for c in range(columns // span):
        picked = slice(c * span, (c + 1) * span)
        full = dot(left_high, high_v[:, picked]) + (dot(left_high, low_v[:, picked]) + dot(left_low, high_v[:, picked]))
        full = full.reshape(count, coarse, span)
        m1 = lax.broadcasted_iota(jnp.int32, (1, coarse, span), 1)
        col = lax.broadcasted_iota(jnp.int32, (1, coarse, span), 2)
        spectral.append(jnp.sum(jnp.where(col % coarse == m1, full, 0.0), axis=1))
    spectral = jnp.concatenate(
        [jnp.concatenate(spectral[:2], axis=1), jnp.concatenate(spectral[2:], axis=1)], axis=0
    ).astype(BF16)
    spectral = jnp.concatenate([spectral, jnp.zeros((tile - 2 * count, orders), BF16)], axis=0)
    coef = dot_t(hot_v[...], spectral).astype(BF16)
    for ty in range(2):
        base = ty * 4 * block
        coef_own[ty] = coef[base : base + block]
        for p in range(1, 4):
            coef_send[ty, p - 1] = coef[base + p * block : base + (p + 1) * block]
    for p in (2, 3, 1):
        for ty in range(2):
            coef_copy(ty, p).start()

    def permute_step(t, carry):
        permute(t)
        return carry

    lax.fori_loop(1, chunks, permute_step, 0)

    source = lax.broadcasted_iota(jnp.int32, (tile, cycles * tile), 0)
    target = lax.broadcasted_iota(jnp.int32, (tile, cycles * tile), 1)
    channel = 2 * ((source // cycles) % maps) + source // count
    same = (source % cycles == target // tile) & (channel == target % channels) & (source < 2 * count)
    expand = jnp.where(same, 1.0, 0.0).astype(BF16)
    depth = 4 * cycles * GROUP
    keep = lax.broadcasted_iota(jnp.int32, (depth, tile), 0) % GROUP == (
        lax.broadcasted_iota(jnp.int32, (depth, tile), 1) // channels
    )
    for ty in range(2):
        spread = []
        for p in range(4):
            if p:
                coef_copy(ty, p).wait_recv()
            values = coef_recv[ty, p - 1] if p else coef_own[ty]
            spread.append(dot(values, expand))
        for g in range(block // GROUP):
            pieces = [
                spread[p][g * GROUP : (g + 1) * GROUP, r * tile : (r + 1) * tile]
                for p in range(4)
                for r in range(cycles)
            ]
            stacked = jnp.where(keep, jnp.concatenate(pieces, axis=0), 0.0)
            lhs_v[ty, g] = stacked.T.astype(BF16)

    groups = block // GROUP
    high_rows = GROUP * channels

    def product(ty, t, g):
        span = slice(g * GROUP, (g + 1) * GROUP)
        parts = [own0[ty, t, :, span, :]] + [recv0[ty, t, p, :, span, :] for p in range(3)]
        right = jnp.concatenate([v.reshape(cycles * GROUP, width) for v in parts], axis=0)
        return dot(lhs_v[ty, g], right)

    def first_step(t):
        for ty in range(2):
            for p in range(1, 4):
                gather_copy(ty, t, p).wait_recv()
            for g in range(groups // 2, groups):
                at_row = (g - groups // 2) * high_rows
                halves[0][ty, t, at_row : at_row + high_rows, :] = product(ty, t, g).astype(BF16)
            half_copy(0, ty, t).start()
        for ty in range(2):
            for g in range(groups // 2):
                acc_v[ty, t, g * high_rows : (g + 1) * high_rows, :] = product(ty, t, g)

    def next_step(s, t):
        size = rows0 >> (s + 1)
        for ty in range(2):
            half_copy(s - 1, ty, t).wait_recv()
            got = halves[2 * s - 1]
            value = acc_v[ty, t, size : 2 * size, :] + got[ty, t, size:, :].astype(F32)
            halves[2 * s][ty, t] = value.astype(BF16)
            half_copy(s, ty, t).start()
            acc_v[ty, t, :size, :] = acc_v[ty, t, :size, :] + got[ty, t, :size, :].astype(F32)

    def pow_copy(u):
        return pltpu.make_async_remote_copy(
            src_ref=pow_v.at[u],
            dst_ref=pow_recv.at[me // sharers],
            send_sem=pow_sems.at[0, u],
            recv_sem=pow_sems.at[1, me // sharers],
            device_id=at(u * sharers + me % sharers),
            device_id_type=MESH,
        )

    def last_step(t):
        size = rows0 >> steps
        ell = t * width + lax.broadcasted_iota(jnp.int32, (channels, width), 1)
        total = [None] * (maps // 2 + 1)
        lanes = pl.ds(pl.multiple_of(t * width, width), width)
        for ty in range(2):
            half_copy(steps - 1, ty, t).wait_recv()
            value = acc_v[ty, t, :size, :] + halves[2 * steps - 1][ty, t].astype(F32)
            for i in range(per_type):
                order = owner_smem[me * own + ty * per_type + i]
                mode = jnp.where(ell >= order, value[i * channels : (i + 1) * channels], 0.0)
                row = (ty * per_type + i) * channels
                harm_ref[row : row + channels, lanes] = mode
                heavy = mode * jnp.where(order == 0, 1.0, 2.0)
                for k in range(maps // 2 + 1):
                    turned = mode if k == 0 else jnp.concatenate([mode[2 * k :], mode[: 2 * k]], axis=0)
                    term = heavy * turned
                    total[k] = term if total[k] is None else total[k] + term
        rows = []
        for i in range(maps):
            for jj in range(i, maps):
                k, a = (jj - i, i) if jj - i <= maps // 2 else (maps - (jj - i), jj)
                rows.append(total[k][2 * a : 2 * a + 1] + total[k][2 * a + 1 : 2 * a + 2])
        power = jnp.concatenate(rows + [jnp.zeros((pow_v.shape[1] - pairs, width), F32)], axis=0)
        for h in range(width // tile):
            u = t * (width // tile) + h
            pow_v[u] = power[:, h * tile : (h + 1) * tile]

            @pl.when(u != me // sharers)
            def _():
                pow_copy(u).start()

    def main(t, carry):
        @pl.when(t < chunks)
        def _():
            first_step(t)

        @pl.when(t > 0)
        def _():
            next_step(1, t - 1)

        return carry

    lax.fori_loop(0, chunks + 1, main, 0)
    for s in range(2, steps):

        def tail(t, carry):
            @pl.when(t < chunks)
            def _():
                next_step(s, t)

            if s == steps - 1:

                @pl.when(t > 0)
                def _():
                    last_step(t - 1)

            return carry

        lax.fori_loop(0, chunks + (s == steps - 1), tail, 0)

    mine = me // sharers
    total = pow_v[mine]
    for u in range(tiles):

        @pl.when(u != mine)
        def _():
            copy = pltpu.make_async_remote_copy(
                src_ref=pow_v.at[u],
                dst_ref=pow_recv.at[u],
                send_sem=pow_sems.at[0, u],
                recv_sem=pow_sems.at[1, u],
                device_id=at(u * sharers + me % sharers),
                device_id_type=MESH,
            )
            copy.wait_recv()

    for u in range(tiles):
        total = total + jnp.where(u != mine, pow_recv[u], 0.0)
    pow_mine[...] = total

    def pair_copy(e):
        return pltpu.make_async_remote_copy(
            src_ref=pow_mine,
            dst_ref=pow_pair.at[e - 1],
            send_sem=pair_sems.at[0, e - 1],
            recv_sem=pair_sems.at[1, e - 1],
            device_id=at(mine * sharers + (me + e) % sharers),
            device_id_type=MESH,
        )

    for e in range(1, sharers):
        pair_copy(e).start()
    for e in range(1, sharers):
        pair_copy(e).wait_recv()
        total = total + pow_pair[e - 1]
    ell = mine * tile + lax.broadcasted_iota(jnp.int32, total.shape, 1)
    total = total / (2 * ell + 1).astype(F32)
    share = tile // sharers
    turned = total
    for c in range(1, sharers):
        shifted = jnp.concatenate([total[:, c * share :], total[:, : c * share]], axis=1)
        turned = jnp.where(me % sharers == c, shifted, turned)
    spec_ref[...] = turned[:pairs, :share]

    def drain(t, carry):
        for ty in range(2):
            for p in range(1, 4):
                gather_copy(ty, t, p).wait_send()
            for s in range(steps):
                half_copy(s, ty, t).wait_send()
        return carry

    lax.fori_loop(0, chunks, drain, 0)
    for ty in range(2):
        for p in range(1, 4):
            coef_copy(ty, p).wait_send()
    for e in range(1, sharers):
        pair_copy(e).wait_send()
    for u in range(tiles):

        @pl.when(u != mine)
        def _():
            pow_copy(u).wait_send()


def per_device(sky_maps, legendre, owner_table):
    maps, cycles, pixels = sky_maps.shape
    _, orders, ells = legendre.shape
    devices = lax.axis_size(AXES)
    grp = lax.axis_size(AXES[1])
    bits = devices.bit_length() - 1
    steps = bits - 2
    width = WIDTH
    chunks = ells // width
    channels = 2 * maps
    own = orders // devices
    block = orders // 8
    tile = 128
    coarse = pixels // tile
    tiles = ells // tile
    sharers = tile * devices // ells
    pairs = maps * (maps + 1) // 2
    padded = -(-pairs // 8) * 8
    first, high, low = fourier_tables(pixels, orders, tile)
    rows0 = block * channels
    halves = []
    for s in range(steps):
        halves += [pltpu.VMEM((2, chunks, rows0 >> (s + 1), width), BF16)] * 2
    cfg = (maps, cycles, orders, ells, devices, grp, width)
    scratch = [
        pltpu.VMEM((chunks, cycles, orders, width), BF16),
        pltpu.VMEM((maps, cycles, coarse, tile), F32),
        pltpu.VMEM(first.shape, F32),
        pltpu.VMEM(high.shape, BF16),
        pltpu.VMEM(low.shape, BF16),
        pltpu.VMEM((orders, orders), BF16),
        pltpu.VMEM((2, block // GROUP, GROUP * channels, 4 * cycles * GROUP), BF16),
        pltpu.VMEM((2, chunks, cycles, block, width), BF16),
        pltpu.VMEM((2, chunks, 3, cycles, block, width), BF16),
        pltpu.VMEM((2, chunks, 3, cycles, block, width), BF16),
        pltpu.VMEM((2, block, tile), BF16),
        pltpu.VMEM((2, 3, block, tile), BF16),
        pltpu.VMEM((2, 3, block, tile), BF16),
        pltpu.VMEM((2, chunks, rows0 // 2, width), F32),
        halves,
        pltpu.VMEM((tiles, padded, tile), F32),
        pltpu.VMEM((tiles, padded, tile), F32),
        pltpu.VMEM((padded, tile), F32),
        pltpu.VMEM((sharers - 1, padded, tile), F32),
        pltpu.SemaphoreType.DMA((chunks,)),
        pltpu.SemaphoreType.DMA((coarse,)),
        pltpu.SemaphoreType.DMA((3,)),
        pltpu.SemaphoreType.DMA((2, 2, chunks, 3)),
        pltpu.SemaphoreType.DMA((2, 2, 3)),
        pltpu.SemaphoreType.DMA((2, steps, 2, chunks)),
        pltpu.SemaphoreType.DMA((2, tiles)),
        pltpu.SemaphoreType.DMA((2, sharers - 1)),
    ]
    anywhere = pl.BlockSpec(memory_space=pl.ANY)
    vmem = pl.BlockSpec(memory_space=pltpu.VMEM)
    harmonics, spectra = pl.pallas_call(
        functools.partial(kernel, cfg),
        out_shape=[
            jax.ShapeDtypeStruct((own * channels, ells), F32),
            jax.ShapeDtypeStruct((pairs, ells // devices), F32),
        ],
        in_specs=[pl.BlockSpec(memory_space=pltpu.SMEM), vmem] + [anywhere] * 5,
        out_specs=[vmem, vmem],
        scratch_shapes=scratch,
        compiler_params=pltpu.CompilerParams(
            vmem_limit_bytes=60 * MIB, collective_id=0, has_side_effects=True
        ),
        cost_estimate=pl.CostEstimate(
            flops=2 * cycles * orders * orders * ells, bytes_accessed=2 * legendre.size, transcendentals=0
        ),
    )(
        owner_table,
        owner_table.reshape(1, orders),
        sky_maps,
        jnp.asarray(first),
        jnp.asarray(high),
        jnp.asarray(low),
        legendre,
    )
    return harmonics.reshape(own, maps, 2, ells), spectra


def solution(mesh):
    return jax.shard_map(
        per_device,
        mesh=mesh,
        in_specs=(P(None, AXES, None), P(AXES, None, None), P()),
        out_specs=(P(AXES, None, None, None), P(None, AXES)),
        check_vma=False,
    )
```

profile of v0, /device:TPU:31, one launch (start us, length us, event | category | flops | bytes accessed | tf_op | source)
XLA Modules:
  0.0 102.1 jit_solution(4225005487441336641)
XLA Ops:
  0.6 97.4 %shard_map.77 = (f32[128,2048]{1,0:T(8,128)}, f32[10,64]{1,0:T(8,128)}) custom-call(s32[512]{0:T(512)} %owner_smem.1, s32[1,512]{1,0:T(1,128)} %bitcast.1, f32[4,4,4096]{2,1,0:T(4,128)} %sky_hbm.1, f32[64,32]{1,0:T(8,128)} %constant.6.clone.first_hbm, bf16[256,1024]{1,0:T(8,128)(2,1)} %constant.7.clone.high_hbm, bf16[256,1024]{1,0:T(8,128)(2,1)} %constant.8.clone.low_hbm, ...), custom_call_target="tpu_custom_call" | custom-call | flops 4294967296 | bytes 8388608 | tf_op jit(solution)/shard_map/pallas_call | solution.py:487
  98.0 2.8 %reshape.11 = f32[16,4,2,2048]{3,2,1,0:T(2,128)} reshape(f32[128,2048]{1,0:T(8,128)} %get-tuple-element.4) | data formatting | bytes 2097152 | tf_op jit(solution)/shard_map/reshape | solution.py:511
  100.9 1.3 %copy.9 = f32[10,64]{1,0:T(8,128)} copy(f32[10,64]{1,0:T(8,128)} %get-tuple-element.9) | data formatting | bytes 5120
where the time goes:
time: 102 us
  Pallas kernels  97.4 us (95%)
  local copies, waits for them, and re-layouts  4.11 us (4%)
    pallas_call x1, Pallas kernels, per_device(): pl.pallas_call(functools.partial(kernel, cfg), out_shape=[jax.ShapeDtypeS...  97.4 us
    reshape x1, local copies, waits for them, and re-layouts, per_device(): return (harmonics.reshape(own, maps, 2, ells), spectra)  2.81 us

commit v1 on v0

--- a/solution.py
+++ b/solution.py
@@ -17,7 +17,9 @@
 GROUP = 16
 FIRST = (1, 2)
 EARLY = 3
-WIDTH = 256
+WIDTH = 128
+AHEAD = 2
+LAGS = (2, 3, 3)
 
 
 def plan_of(bits):
@@ -124,19 +126,19 @@
         table.start()
 
     j = lax.broadcasted_iota(jnp.int32, (orders, tile), 0)
-    part = j // (orders // 2)
-    rest = j % block
-    slot = part * per_type + rest % per_type
+    half_bit, block_bit = (orders // 2).bit_length() - 1, block.bit_length() - 1
+    part = j >> half_bit
+    slot = part * per_type + (j & (per_type - 1))
 
     def place(b, differs):
         mine = bit(b)
         return (mine + differs - 2 * mine * differs) * ((1 << b) * own)
 
-    slot = slot + place(0, (j // block) % 2)
+    slot = slot + place(0, (j >> block_bit) & 1)
     for ty in range(2):
-        terms = place(FIRST[ty], (j // (2 * block)) % 2)
+        terms = place(FIRST[ty], (j >> (block_bit + 1)) & 1)
         for s, b in enumerate(later[ty]):
-            terms = terms + place(b, (rest // (block >> (s + 1))) % 2)
+            terms = terms + place(b, (j >> (block_bit - s - 1)) & 1)
         slot = slot + jnp.where(part == ty, terms, 0)
     lane = lax.broadcasted_iota(jnp.int32, (orders, tile), 1)
     pick = jnp.concatenate(
@@ -176,26 +178,36 @@
         )
 
     def permute(t):
-        load(t).wait()
-        for r in range(cycles):
-            values = leg_v[t, r]
+        with jax.named_scope("load"):
+            load(t).wait()
+        with jax.named_scope("permute"):
+            permute_loaded(t)
+
+    def permute_loaded(t):
+        together = max(1, 256 // width)
+        for r0 in range(0, cycles, together):
+            values = jnp.concatenate([leg_v[t, r0 + i] for i in range(together)], axis=1)
             for ty in range(2):
                 picked = dot(hot_v[ty * 4 * block : (ty + 1) * 4 * block, :], values).astype(BF16)
-                own0[ty, t, r] = picked[:block]
-                for p in range(1, 4):
-                    send0[ty, t, p - 1, r] = picked[p * block : (p + 1) * block]
+                for i in range(together):
+                    piece = picked[:, i * width : (i + 1) * width]
+                    own0[ty, t, r0 + i] = piece[:block]
+                    for p in range(1, 4):
+                        send0[ty, t, p - 1, r0 + i] = piece[p * block : (p + 1) * block]
         for p in (2, 3, 1):
             for ty in range(2):
                 gather_copy(ty, t, p).start()
 
-    pl.semaphore_wait(barrier, len(near))
+    with jax.named_scope("barrier"):
+        pl.semaphore_wait(barrier, len(near))
     permute(0)
 
     def sky_wait(k, carry):
         sky_load(k).wait()
         return carry
 
-    lax.fori_loop(0, coarse, sky_wait, 0)
+    with jax.named_scope("waitsky"):
+        lax.fori_loop(0, coarse, sky_wait, 0)
     for table in tables:
         table.wait()
     count = maps * cycles
@@ -235,7 +247,7 @@
         permute(t)
         return carry
 
-    lax.fori_loop(1, chunks, permute_step, 0)
+    lax.fori_loop(1, AHEAD + 1, permute_step, 0)
 
     source = lax.broadcasted_iota(jnp.int32, (tile, cycles * tile), 0)
     target = lax.broadcasted_iota(jnp.int32, (tile, cycles * tile), 1)
@@ -250,7 +262,8 @@
         spread = []
         for p in range(4):
             if p:
-                coef_copy(ty, p).wait_recv()
+                with jax.named_scope("waitcoef"):
+                    coef_copy(ty, p).wait_recv()
             values = coef_recv[ty, p - 1] if p else coef_own[ty]
             spread.append(dot(values, expand))
         for g in range(block // GROUP):
@@ -273,8 +286,9 @@
 
     def first_step(t):
         for ty in range(2):
-            for p in range(1, 4):
-                gather_copy(ty, t, p).wait_recv()
+            with jax.named_scope("wait0"):
+                for p in range(1, 4):
+                    gather_copy(ty, t, p).wait_recv()
             for g in range(groups // 2, groups):
                 at_row = (g - groups // 2) * high_rows
                 halves[0][ty, t, at_row : at_row + high_rows, :] = product(ty, t, g).astype(BF16)
@@ -286,7 +300,8 @@
     def next_step(s, t):
         size = rows0 >> (s + 1)
         for ty in range(2):
-            half_copy(s - 1, ty, t).wait_recv()
+            with jax.named_scope(f"wait{s}"):
+                half_copy(s - 1, ty, t).wait_recv()
             got = halves[2 * s - 1]
             value = acc_v[ty, t, size : 2 * size, :] + got[ty, t, size:, :].astype(F32)
             halves[2 * s][ty, t] = value.astype(BF16)
@@ -309,13 +324,15 @@
         total = [None] * (maps // 2 + 1)
         lanes = pl.ds(pl.multiple_of(t * width, width), width)
         for ty in range(2):
-            half_copy(steps - 1, ty, t).wait_recv()
+            with jax.named_scope("waitlast"):
+                half_copy(steps - 1, ty, t).wait_recv()
             value = acc_v[ty, t, :size, :] + halves[2 * steps - 1][ty, t].astype(F32)
             for i in range(per_type):
                 order = owner_smem[me * own + ty * per_type + i]
                 mode = jnp.where(ell >= order, value[i * channels : (i + 1) * channels], 0.0)
-                row = (ty * per_type + i) * channels
-                harm_ref[row : row + channels, lanes] = mode
+                row = (ty * per_type + i) * maps
+                for a in range(maps):
+                    harm_ref[row + a, :, lanes] = mode[2 * a : 2 * a + 2]
                 heavy = mode * jnp.where(order == 0, 1.0, 2.0)
                 for k in range(maps // 2 + 1):
                     turned = mode if k == 0 else jnp.concatenate([mode[2 * k :], mode[: 2 * k]], axis=0)
@@ -335,34 +352,36 @@
             def _():
                 pow_copy(u).start()
 
+    lags = [0, LAGS[0]]
+    for s in range(2, steps):
+        lags.append(lags[-1] + LAGS[1])
+    end = lags[-1] + LAGS[2]
+
     def main(t, carry):
+        @pl.when((t > 0) & (t + AHEAD < chunks))
+        def _():
+            permute(t + AHEAD)
+
         @pl.when(t < chunks)
         def _():
-            first_step(t)
-
-        @pl.when(t > 0)
+            with jax.named_scope("first"):
+                first_step(t)
+
+        for s in range(1, steps):
+
+            @pl.when((t >= lags[s]) & (t < chunks + lags[s]))
+            def _():
+                with jax.named_scope(f"next{s}"):
+                    next_step(s, t - lags[s])
+
+        @pl.when(t >= end)
         def _():
-            next_step(1, t - 1)
+            with jax.named_scope("last"):
+                last_step(t - end)
 
         return carry
 
-    lax.fori_loop(0, chunks + 1, main, 0)
-    for s in range(2, steps):
-
-        def tail(t, carry):
-            @pl.when(t < chunks)
-            def _():
-                next_step(s, t)
-
-            if s == steps - 1:
-
-                @pl.when(t > 0)
-                def _():
-                    last_step(t - 1)
-
-            return carry
-
-        lax.fori_loop(0, chunks + (s == steps - 1), tail, 0)
+    lax.fori_loop(0, chunks + end, main, 0)
 
     mine = me // sharers
     total = pow_v[mine]
@@ -378,7 +397,8 @@
                 device_id=at(u * sharers + me % sharers),
                 device_id_type=MESH,
             )
-            copy.wait_recv()
+            with jax.named_scope("waitpow"):
+                copy.wait_recv()
 
     for u in range(tiles):
         total = total + jnp.where(u != mine, pow_recv[u], 0.0)
@@ -397,7 +417,8 @@
     for e in range(1, sharers):
         pair_copy(e).start()
     for e in range(1, sharers):
-        pair_copy(e).wait_recv()
+        with jax.named_scope("waitpair"):
+            pair_copy(e).wait_recv()
         total = total + pow_pair[e - 1]
     ell = mine * tile + lax.broadcasted_iota(jnp.int32, total.shape, 1)
     total = total / (2 * ell + 1).astype(F32)
@@ -416,7 +437,8 @@
                 half_copy(s, ty, t).wait_send()
         return carry
 
-    lax.fori_loop(0, chunks, drain, 0)
+    with jax.named_scope("drain"):
+        lax.fori_loop(0, chunks, drain, 0)
     for ty in range(2):
         for p in range(1, 4):
             coef_copy(ty, p).wait_send()
@@ -487,7 +509,7 @@
     harmonics, spectra = pl.pallas_call(
         functools.partial(kernel, cfg),
         out_shape=[
-            jax.ShapeDtypeStruct((own * channels, ells), F32),
+            jax.ShapeDtypeStruct((own * maps, 2, ells), F32),
             jax.ShapeDtypeStruct((pairs, ells // devices), F32),
         ],
         in_specs=[pl.BlockSpec(memory_space=pltpu.SMEM), vmem] + [anywhere] * 5,

time: 102 us -> 89.9 us (0.88)
  Pallas kernels: 97.4 us -> 85.5 us
    pallas_call x1, Pallas kernels: 97.4 us -> 85.5 us  [per_device(): pl.pallas_call(functools.partial(kernel, cfg), out_shape=[jax.ShapeDtypeS...]
    reshape x1 -> x0, local copies, waits for them, and re-layouts: 2.81 us -> none  [per_device(): return (harmonics.reshape(own, maps, 2, ells), spectra)]
    unnamed x1 -> x2, local copies, waits for them, and re-layouts: 1.29 us -> 3.58 us
where the time goes in v1:
time: 89.9 us; the launch traced here: 89.7 us
  Pallas kernels  85.5 us (95%)
  local copies, waits for them, and re-layouts  3.58 us (4%)
    pallas_call x1, Pallas kernels, per_device(): pl.pallas_call(functools.partial(kernel, cfg), out_shape=[jax.ShapeDtypeS...  85.5 us
    unnamed x2, local copies, waits for them, and re-layouts  3.58 us

profile of v1, /device:TPU:31, one launch (start us, length us, event | category | flops | bytes accessed | tf_op | source)
XLA Modules:
  0.0 89.7 jit_solution(17217730496422642373)
XLA Ops:
  0.6 85.5 %shard_map.77 = (f32[64,2,2048]{2,1,0:T(2,128)}, f32[10,64]{1,0:T(8,128)}) custom-call(s32[512]{0:T(512)} %owner_smem.1, s32[1,512]{1,0:T(1,128)} %bitcast.3, f32[4,4,4096]{2,1,0:T(4,128)} %sky_hbm.1, f32[64,32]{1,0:T(8,128)} %constant.6.clone.first_hbm, bf16[256,1024]{1,0:T(8,128)(2,1)} %constant.7.clone.high_hbm, bf16[256,1024]{1,0:T(8,128)(2,1)} %constant.8.clone.low_hbm, ...), custom_call_target="tpu_custom_call" | custom-call | flops 4294967296 | bytes 8388608 | tf_op jit(solution)/shard_map/pallas_call | solution.py:509
  86.1 2.3 %copy.10 = f32[16,4,2,2048]{3,2,1,0:T(2,128)} copy(f32[16,4,2,2048]{3,2,1,0:T(2,128)} %bitcast.2) | data formatting | bytes 2097152
  88.4 1.3 %copy.11 = f32[10,64]{1,0:T(8,128)} copy(f32[10,64]{1,0:T(8,128)} %get-tuple-element.9) | data formatting | bytes 5120

commit v2 on v1

--- a/solution.py
+++ b/solution.py
@@ -18,8 +18,10 @@
 FIRST = (1, 2)
 EARLY = 3
 WIDTH = 128
-AHEAD = 2
-LAGS = (2, 3, 3)
+AHEAD = 3
+SWAPPED = 1
+SLOTS = 10
+LAGS = (3, 3, 4)
 
 
 def plan_of(bits):
@@ -66,8 +68,8 @@
 def kernel(
     cfg, owner_smem, owner_ref, sky_hbm, first_hbm, high_hbm, low_hbm, leg_hbm, harm_ref, spec_ref,
     leg_v, sky_v, first_v, high_v, low_v, hot_v, lhs_v, own0, send0, recv0, coef_own, coef_send, coef_recv,
-    acc_v, halves, pow_v, pow_recv, pow_mine, pow_pair, load_sem, sky_sem, table_sem,
-    sems0, coef_sems, half_sems, pow_sems, pair_sems,
+    acc_v, halves, harm_v, pow_v, pow_recv, pow_mine, pow_pair, load_sem, sky_sem, table_sem,
+    sent_sems, sems0, coef_sems, half_sems, harm_sem, pow_sem, pair_sems,
 ):
     maps, cycles, orders, ells, devices, grp, width = cfg
     bits = devices.bit_length() - 1
@@ -94,30 +96,33 @@
     gather = [[None, flip(me, [0]), flip(me, [FIRST[ty]]), flip(me, [FIRST[ty], 0])] for ty in range(2)]
     near = sorted({(0,)} | {(f,) for f in FIRST} | {(0, f) for f in FIRST} | {(b,) for b in range(1, bits)})
 
+    scope = jax.named_scope
     barrier = pltpu.get_barrier_semaphore()
     for masks in near:
         pl.semaphore_signal(barrier, inc=1, device_id=at(flip(me, masks)), device_id_type=MESH)
 
     def load(t):
         lanes = pl.ds(pl.multiple_of(t * width, width), width)
-        return pltpu.make_async_copy(leg_hbm.at[:, :, lanes], leg_v.at[t], load_sem.at[t])
+        return pltpu.make_async_copy(leg_hbm.at[:, :, lanes], leg_v.at[t], load_sem.at[t % 4])
 
     def load_start(t, carry):
         load(t).start()
         return carry
 
-    lax.fori_loop(0, chunks, load_start, 0)
+    with scope("startload"):
+        lax.fori_loop(0, 4, load_start, 0)
     coarse = sky_v.shape[2]
 
     def sky_load(k):
         lanes = pl.ds(pl.multiple_of(k * tile, tile), tile)
-        return pltpu.make_async_copy(sky_hbm.at[:, :, lanes], sky_v.at[:, :, k, :], sky_sem.at[k])
+        return pltpu.make_async_copy(sky_hbm.at[:, :, lanes], sky_v.at[:, :, k, :], sky_sem)
 
     def sky_start(k, carry):
         sky_load(k).start()
         return carry
 
-    lax.fori_loop(0, coarse, sky_start, 0)
+    with scope("startsky"):
+        lax.fori_loop(0, coarse, sky_start, 0)
     tables = [
         pltpu.make_async_copy(src, dst, table_sem.at[i])
         for i, (src, dst) in enumerate(((first_hbm, first_v), (high_hbm, high_v), (low_hbm, low_v)))
@@ -147,12 +152,15 @@
     table = jnp.where(lax.broadcasted_iota(jnp.int32, (orders, orders), 0) == owner_ref[...], 1.0, 0.0).astype(BF16)
     hot_v[...] = dot_t(pick, table).astype(BF16)
 
+    def whole(ref, sem):
+        return pltpu.make_async_copy(ref, ref, sem)
+
     def gather_copy(ty, t, p):
         return pltpu.make_async_remote_copy(
             src_ref=send0.at[ty, t, p - 1],
             dst_ref=recv0.at[ty, t, p - 1],
-            send_sem=sems0.at[0, ty, t, p - 1],
-            recv_sem=sems0.at[1, ty, t, p - 1],
+            send_sem=sent_sems.at[0],
+            recv_sem=sems0.at[t % SLOTS, ty],
             device_id=at(gather[ty][p]),
             device_id_type=MESH,
         )
@@ -161,19 +169,25 @@
         return pltpu.make_async_remote_copy(
             src_ref=coef_send.at[ty, p - 1],
             dst_ref=coef_recv.at[ty, p - 1],
-            send_sem=coef_sems.at[0, ty, p - 1],
-            recv_sem=coef_sems.at[1, ty, p - 1],
+            send_sem=sent_sems.at[1],
+            recv_sem=coef_sems.at[ty],
             device_id=at(gather[ty][p]),
             device_id_type=MESH,
         )
 
+    swap_from = chunks - SWAPPED
+    groups = block // GROUP
+
     def half_copy(s, ty, t):
+        partner = flip(me, [later[ty][s]])
+        if s < 2:
+            partner = jnp.where(t < swap_from, partner, flip(me, [later[ty][1 - s]]))
         return pltpu.make_async_remote_copy(
             src_ref=halves[2 * s].at[ty, t],
             dst_ref=halves[2 * s + 1].at[ty, t],
-            send_sem=half_sems.at[0, s, ty, t],
-            recv_sem=half_sems.at[1, s, ty, t],
-            device_id=at(flip(me, [later[ty][s]])),
+            send_sem=sent_sems.at[2 + s],
+            recv_sem=half_sems.at[s, t % SLOTS, ty],
+            device_id=at(partner),
             device_id_type=MESH,
         )
 
@@ -182,6 +196,10 @@
             load(t).wait()
         with jax.named_scope("permute"):
             permute_loaded(t)
+
+        @pl.when(t + 4 < chunks)
+        def _():
+            load(t + 4).start()
 
     def permute_loaded(t):
         together = max(1, 256 // width)
@@ -202,12 +220,8 @@
         pl.semaphore_wait(barrier, len(near))
     permute(0)
 
-    def sky_wait(k, carry):
-        sky_load(k).wait()
-        return carry
-
     with jax.named_scope("waitsky"):
-        lax.fori_loop(0, coarse, sky_wait, 0)
+        whole(sky_v, sky_sem).wait()
     for table in tables:
         table.wait()
     count = maps * cycles
@@ -260,10 +274,9 @@
     )
     for ty in range(2):
         spread = []
+        with jax.named_scope("waitcoef"):
+            whole(coef_recv.at[ty], coef_sems.at[ty]).wait()
         for p in range(4):
-            if p:
-                with jax.named_scope("waitcoef"):
-                    coef_copy(ty, p).wait_recv()
             values = coef_recv[ty, p - 1] if p else coef_own[ty]
             spread.append(dot(values, expand))
         for g in range(block // GROUP):
@@ -275,7 +288,6 @@
             stacked = jnp.where(keep, jnp.concatenate(pieces, axis=0), 0.0)
             lhs_v[ty, g] = stacked.T.astype(BF16)
 
-    groups = block // GROUP
     high_rows = GROUP * channels
 
     def product(ty, t, g):
@@ -284,18 +296,16 @@
         right = jnp.concatenate([v.reshape(cycles * GROUP, width) for v in parts], axis=0)
         return dot(lhs_v[ty, g], right)
 
-    def first_step(t):
+    def first_step(t, sent, kept):
         for ty in range(2):
             with jax.named_scope("wait0"):
-                for p in range(1, 4):
-                    gather_copy(ty, t, p).wait_recv()
-            for g in range(groups // 2, groups):
-                at_row = (g - groups // 2) * high_rows
-                halves[0][ty, t, at_row : at_row + high_rows, :] = product(ty, t, g).astype(BF16)
+                whole(recv0.at[ty, t], sems0.at[t % SLOTS, ty]).wait()
+            for i, g in enumerate(sent):
+                halves[0][ty, t, i * high_rows : (i + 1) * high_rows, :] = product(ty, t, g).astype(BF16)
             half_copy(0, ty, t).start()
         for ty in range(2):
-            for g in range(groups // 2):
-                acc_v[ty, t, g * high_rows : (g + 1) * high_rows, :] = product(ty, t, g)
+            for i, g in enumerate(kept):
+                acc_v[ty, t, i * high_rows : (i + 1) * high_rows, :] = product(ty, t, g)
 
     def next_step(s, t):
         size = rows0 >> (s + 1)
@@ -312,17 +322,20 @@
         return pltpu.make_async_remote_copy(
             src_ref=pow_v.at[u],
             dst_ref=pow_recv.at[me // sharers],
-            send_sem=pow_sems.at[0, u],
-            recv_sem=pow_sems.at[1, me // sharers],
+            send_sem=sent_sems.at[2 + steps],
+            recv_sem=pow_sem,
             device_id=at(u * sharers + me % sharers),
             device_id_type=MESH,
         )
+
+    def harm_copy(t):
+        lanes = pl.ds(pl.multiple_of(t * width, width), width)
+        return pltpu.make_async_copy(harm_v.at[t], harm_ref.at[:, :, lanes], harm_sem)
 
     def last_step(t):
         size = rows0 >> steps
         ell = t * width + lax.broadcasted_iota(jnp.int32, (channels, width), 1)
         total = [None] * (maps // 2 + 1)
-        lanes = pl.ds(pl.multiple_of(t * width, width), width)
         for ty in range(2):
             with jax.named_scope("waitlast"):
                 half_copy(steps - 1, ty, t).wait_recv()
@@ -332,12 +345,13 @@
                 mode = jnp.where(ell >= order, value[i * channels : (i + 1) * channels], 0.0)
                 row = (ty * per_type + i) * maps
                 for a in range(maps):
-                    harm_ref[row + a, :, lanes] = mode[2 * a : 2 * a + 2]
+                    harm_v[t, row + a] = mode[2 * a : 2 * a + 2]
                 heavy = mode * jnp.where(order == 0, 1.0, 2.0)
                 for k in range(maps // 2 + 1):
                     turned = mode if k == 0 else jnp.concatenate([mode[2 * k :], mode[: 2 * k]], axis=0)
                     term = heavy * turned
                     total[k] = term if total[k] is None else total[k] + term
+        harm_copy(t).start()
         rows = []
         for i in range(maps):
             for jj in range(i, maps):
@@ -362,10 +376,15 @@
         def _():
             permute(t + AHEAD)
 
-        @pl.when(t < chunks)
+        @pl.when(t < swap_from)
         def _():
             with jax.named_scope("first"):
-                first_step(t)
+                first_step(t, (2, 3), (0, 1))
+
+        @pl.when((t >= swap_from) & (t < chunks))
+        def _():
+            with jax.named_scope("first"):
+                first_step(t, (1, 3), (0, 2))
 
         for s in range(1, steps):
 
@@ -385,21 +404,8 @@
 
     mine = me // sharers
     total = pow_v[mine]
-    for u in range(tiles):
-
-        @pl.when(u != mine)
-        def _():
-            copy = pltpu.make_async_remote_copy(
-                src_ref=pow_v.at[u],
-                dst_ref=pow_recv.at[u],
-                send_sem=pow_sems.at[0, u],
-                recv_sem=pow_sems.at[1, u],
-                device_id=at(u * sharers + me % sharers),
-                device_id_type=MESH,
-            )
-            with jax.named_scope("waitpow"):
-                copy.wait_recv()
-
+    with scope("waitpow"):
+        whole(pow_recv.at[: tiles - 1], pow_sem).wait()
     for u in range(tiles):
         total = total + jnp.where(u != mine, pow_recv[u], 0.0)
     pow_mine[...] = total
@@ -429,26 +435,51 @@
         turned = jnp.where(me % sharers == c, shifted, turned)
     spec_ref[...] = turned[:pairs, :share]
 
-    def drain(t, carry):
-        for ty in range(2):
-            for p in range(1, 4):
-                gather_copy(ty, t, p).wait_send()
-            for s in range(steps):
-                half_copy(s, ty, t).wait_send()
-        return carry
-
     with jax.named_scope("drain"):
-        lax.fori_loop(0, chunks, drain, 0)
-    for ty in range(2):
-        for p in range(1, 4):
-            coef_copy(ty, p).wait_send()
+        whole(harm_v, harm_sem).wait()
+        whole(send0, sent_sems.at[0]).wait()
+        whole(coef_send, sent_sems.at[1]).wait()
+        for s in range(steps):
+            whole(halves[2 * s], sent_sems.at[2 + s]).wait()
     for e in range(1, sharers):
         pair_copy(e).wait_send()
-    for u in range(tiles):
-
-        @pl.when(u != mine)
-        def _():
-            pow_copy(u).wait_send()
+    whole(pow_v.at[: tiles - 1], sent_sems.at[2 + steps]).wait()
+
+
+def hand_over_body(parts, large_ref, small_ref, large_out, small_out, large_v, small_v, sems, small_sems):
+    rows = large_v.shape[0] // parts
+    ins, outs = [], []
+    for c in range(parts):
+        picked = slice(c * rows, (c + 1) * rows)
+        ins.append(pltpu.make_async_copy(large_ref.at[picked], large_v.at[picked], sems.at[0, c]))
+        outs.append(pltpu.make_async_copy(large_v.at[picked], large_out.at[picked], sems.at[1, c]))
+    ins.append(pltpu.make_async_copy(small_ref, small_v, small_sems.at[0]))
+    outs.append(pltpu.make_async_copy(small_v, small_out, small_sems.at[1]))
+    for copy in ins:
+        copy.start()
+    for got, put in zip(ins, outs):
+        got.wait()
+        put.start()
+    for copy in outs:
+        copy.wait()
+
+
+def hand_over(large, small):
+    parts = 4
+    anywhere = pl.BlockSpec(memory_space=pl.ANY)
+    return pl.pallas_call(
+        functools.partial(hand_over_body, parts),
+        out_shape=[jax.ShapeDtypeStruct(large.shape, large.dtype), jax.ShapeDtypeStruct(small.shape, small.dtype)],
+        in_specs=[anywhere] * 2,
+        out_specs=[anywhere] * 2,
+        scratch_shapes=[
+            pltpu.VMEM(large.shape, large.dtype),
+            pltpu.VMEM(small.shape, small.dtype),
+            pltpu.SemaphoreType.DMA((2, parts)),
+            pltpu.SemaphoreType.DMA((2,)),
+        ],
+        cost_estimate=pl.CostEstimate(flops=large.size, bytes_accessed=8 * large.size, transcendentals=0),
+    )(large, small)
 
 
 def per_device(sky_maps, legendre, owner_table):
@@ -491,17 +522,20 @@
         pltpu.VMEM((2, 3, block, tile), BF16),
         pltpu.VMEM((2, chunks, rows0 // 2, width), F32),
         halves,
+        pltpu.VMEM((chunks, own * maps, 2, width), F32),
         pltpu.VMEM((tiles, padded, tile), F32),
         pltpu.VMEM((tiles, padded, tile), F32),
         pltpu.VMEM((padded, tile), F32),
         pltpu.VMEM((sharers - 1, padded, tile), F32),
-        pltpu.SemaphoreType.DMA((chunks,)),
-        pltpu.SemaphoreType.DMA((coarse,)),
+        pltpu.SemaphoreType.DMA((4,)),
+        pltpu.SemaphoreType.DMA,
         pltpu.SemaphoreType.DMA((3,)),
-        pltpu.SemaphoreType.DMA((2, 2, chunks, 3)),
-        pltpu.SemaphoreType.DMA((2, 2, 3)),
-        pltpu.SemaphoreType.DMA((2, steps, 2, chunks)),
-        pltpu.SemaphoreType.DMA((2, tiles)),
+        pltpu.SemaphoreType.DMA((3 + steps,)),
+        pltpu.SemaphoreType.DMA((SLOTS, 2)),
+        pltpu.SemaphoreType.DMA((2,)),
+        pltpu.SemaphoreType.DMA((steps, SLOTS, 2)),
+        pltpu.SemaphoreType.DMA,
+        pltpu.SemaphoreType.DMA,
         pltpu.SemaphoreType.DMA((2, sharers - 1)),
     ]
     anywhere = pl.BlockSpec(memory_space=pl.ANY)
@@ -513,7 +547,7 @@
             jax.ShapeDtypeStruct((pairs, ells // devices), F32),
         ],
         in_specs=[pl.BlockSpec(memory_space=pltpu.SMEM), vmem] + [anywhere] * 5,
-        out_specs=[vmem, vmem],
+        out_specs=[anywhere, vmem],
         scratch_shapes=scratch,
         compiler_params=pltpu.CompilerParams(
             vmem_limit_bytes=60 * MIB, collective_id=0, has_side_effects=True
@@ -530,6 +564,7 @@
         jnp.asarray(low),
         legendre,
     )
+    harmonics, spectra = hand_over(harmonics, spectra)
     return harmonics.reshape(own, maps, 2, ells), spectra
 
 

time: 89.9 us -> 81.7 us (0.909)
  Pallas kernels: 85.5 us -> 80.4 us
  local copies, waits for them, and re-layouts: 3.58 us -> 0 us
    pallas_call x1, Pallas kernels: 85.5 us -> 78.4 us  [per_device(): pl.pallas_call(functools.partial(kernel, cfg), out_shape=[jax.ShapeDtypeS...]
    unnamed x2 -> x0, local copies, waits for them, and re-layouts: 3.58 us -> none
    pallas_call x0 -> x1, Pallas kernels: none -> 2 us  [hand_over(): pl.pallas_call(functools.partial(hand_over_body, parts), out_shape=[jax.S...]
where the time goes in v2:
time: 81.7 us; the launch traced here: 81 us
  Pallas kernels  80.4 us (98%)
    pallas_call x1, Pallas kernels, per_device(): pl.pallas_call(functools.partial(kernel, cfg), out_shape=[jax.ShapeDtypeS...  78.4 us
    pallas_call x1, Pallas kernels, hand_over(): pl.pallas_call(functools.partial(hand_over_body, parts), out_shape=[jax.S...  2 us

profile of v2, /device:TPU:31, one launch (start us, length us, event | category | flops | bytes accessed | tf_op | source)
XLA Modules:
  0.0 81.0 jit_solution(4410879436844560781)
XLA Ops:
  0.6 78.4 %shard_map.77 = (f32[64,2,2048]{2,1,0:T(2,128)}, f32[10,64]{1,0:T(8,128)}) custom-call(s32[512]{0:T(512)} %owner_smem.1, s32[1,512]{1,0:T(1,128)} %bitcast.3, f32[4,4,4096]{2,1,0:T(4,128)} %sky_hbm.1, f32[64,32]{1,0:T(8,128)} %constant.6.clone.first_hbm, bf16[256,1024]{1,0:T(8,128)(2,1)} %constant.7.clone.high_hbm, bf16[256,1024]{1,0:T(8,128)(2,1)} %constant.8.clone.low_hbm, ...), custom_call_target="tpu_custom_call" | custom-call | flops 4294967296 | bytes 8388608 | tf_op jit(solution)/shard_map/pallas_call | solution.py:543
  79.0 2.0 %shard_map.78 = (f32[64,2,2048]{2,1,0:T(2,128)}, f32[10,64]{1,0:T(8,128)}) custom-call(f32[64,2,2048]{2,1,0:T(2,128)} %get-tuple-element.6.large_ref, f32[10,64]{1,0:T(8,128)} %get-tuple-element.7.small_ref), custom_call_target="tpu_custom_call" | custom-call | flops 262144 | bytes 2097152 | tf_op jit(solution)/shard_map/pallas_call | solution.py:470

commit v3 on v2

--- a/solution.py
+++ b/solution.py
@@ -19,9 +19,9 @@
 EARLY = 3
 WIDTH = 128
 AHEAD = 3
-SWAPPED = 1
-SLOTS = 10
-LAGS = (3, 3, 4)
+SWAPPED = 2
+SLOTS = 8
+LAGS = (2, 2, 3)
 
 
 def plan_of(bits):
@@ -66,10 +66,10 @@
 
 
 def kernel(
-    cfg, owner_smem, owner_ref, sky_hbm, first_hbm, high_hbm, low_hbm, leg_hbm, harm_ref, spec_ref,
-    leg_v, sky_v, first_v, high_v, low_v, hot_v, lhs_v, own0, send0, recv0, coef_own, coef_send, coef_recv,
-    acc_v, halves, harm_v, pow_v, pow_recv, pow_mine, pow_pair, load_sem, sky_sem, table_sem,
-    sent_sems, sems0, coef_sems, half_sems, harm_sem, pow_sem, pair_sems,
+    cfg, owner_hbm, owner_row_hbm, sky_hbm, first_hbm, high_hbm, low_hbm, leg_hbm, harm_ref, spec_ref,
+    owner_smem, owner_ref, leg_v, sky_v, first_v, high_v, low_v, hot_v, lhs_v, own0, send0, recv0, coef_own, coef_send, coef_recv,
+    acc_v, halves, pow_v, pow_recv, pow_mine, pow_pair, load_sem, sky_sem, table_sem,
+    sent_sems, sems0, coef_sems, half_sems, pow_sem, pair_sems,
 ):
     maps, cycles, orders, ells, devices, grp, width = cfg
     bits = devices.bit_length() - 1
@@ -97,6 +97,8 @@
     near = sorted({(0,)} | {(f,) for f in FIRST} | {(0, f) for f in FIRST} | {(b,) for b in range(1, bits)})
 
     scope = jax.named_scope
+    row_load = pltpu.make_async_copy(owner_row_hbm, owner_ref, table_sem.at[3])
+    row_load.start()
     barrier = pltpu.get_barrier_semaphore()
     for masks in near:
         pl.semaphore_signal(barrier, inc=1, device_id=at(flip(me, masks)), device_id_type=MESH)
@@ -114,21 +116,18 @@
     coarse = sky_v.shape[2]
 
     def sky_load(k):
-        lanes = pl.ds(pl.multiple_of(k * tile, tile), tile)
+        lanes = pl.ds(k * tile, tile)
         return pltpu.make_async_copy(sky_hbm.at[:, :, lanes], sky_v.at[:, :, k, :], sky_sem)
 
-    def sky_start(k, carry):
+    for k in range(coarse):
         sky_load(k).start()
-        return carry
-
-    with scope("startsky"):
-        lax.fori_loop(0, coarse, sky_start, 0)
     tables = [
         pltpu.make_async_copy(src, dst, table_sem.at[i])
         for i, (src, dst) in enumerate(((first_hbm, first_v), (high_hbm, high_v), (low_hbm, low_v)))
     ]
     for table in tables:
         table.start()
+
 
     j = lax.broadcasted_iota(jnp.int32, (orders, tile), 0)
     half_bit, block_bit = (orders // 2).bit_length() - 1, block.bit_length() - 1
@@ -149,6 +148,7 @@
     pick = jnp.concatenate(
         [jnp.where(slot == lane + c * tile, 1.0, 0.0).astype(BF16) for c in range(orders // tile)], axis=1
     )
+    row_load.wait()
     table = jnp.where(lax.broadcasted_iota(jnp.int32, (orders, orders), 0) == owner_ref[...], 1.0, 0.0).astype(BF16)
     hot_v[...] = dot_t(pick, table).astype(BF16)
 
@@ -219,6 +219,8 @@
     with jax.named_scope("barrier"):
         pl.semaphore_wait(barrier, len(near))
     permute(0)
+    order_load = pltpu.make_async_copy(owner_hbm, owner_smem, table_sem.at[4])
+    order_load.start()
 
     with jax.named_scope("waitsky"):
         whole(sky_v, sky_sem).wait()
@@ -257,6 +259,8 @@
         for ty in range(2):
             coef_copy(ty, p).start()
 
+    order_load.wait()
+
     def permute_step(t, carry):
         permute(t)
         return carry
@@ -328,14 +332,11 @@
             device_id_type=MESH,
         )
 
-    def harm_copy(t):
-        lanes = pl.ds(pl.multiple_of(t * width, width), width)
-        return pltpu.make_async_copy(harm_v.at[t], harm_ref.at[:, :, lanes], harm_sem)
-
     def last_step(t):
         size = rows0 >> steps
         ell = t * width + lax.broadcasted_iota(jnp.int32, (channels, width), 1)
         total = [None] * (maps // 2 + 1)
+        lanes = pl.ds(pl.multiple_of(t * width, width), width)
         for ty in range(2):
             with jax.named_scope("waitlast"):
                 half_copy(steps - 1, ty, t).wait_recv()
@@ -345,19 +346,18 @@
                 mode = jnp.where(ell >= order, value[i * channels : (i + 1) * channels], 0.0)
                 row = (ty * per_type + i) * maps
                 for a in range(maps):
-                    harm_v[t, row + a] = mode[2 * a : 2 * a + 2]
+                    harm_ref[row + a, :, lanes] = mode[2 * a : 2 * a + 2]
                 heavy = mode * jnp.where(order == 0, 1.0, 2.0)
                 for k in range(maps // 2 + 1):
                     turned = mode if k == 0 else jnp.concatenate([mode[2 * k :], mode[: 2 * k]], axis=0)
                     term = heavy * turned
                     total[k] = term if total[k] is None else total[k] + term
-        harm_copy(t).start()
         rows = []
         for i in range(maps):
             for jj in range(i, maps):
                 k, a = (jj - i, i) if jj - i <= maps // 2 else (maps - (jj - i), jj)
                 rows.append(total[k][2 * a : 2 * a + 1] + total[k][2 * a + 1 : 2 * a + 2])
-        power = jnp.concatenate(rows + [jnp.zeros((pow_v.shape[1] - pairs, width), F32)], axis=0)
+        power = jnp.concatenate(rows, axis=0)
         for h in range(width // tile):
             u = t * (width // tile) + h
             pow_v[u] = power[:, h * tile : (h + 1) * tile]
@@ -433,10 +433,9 @@
     for c in range(1, sharers):
         shifted = jnp.concatenate([total[:, c * share :], total[:, : c * share]], axis=1)
         turned = jnp.where(me % sharers == c, shifted, turned)
-    spec_ref[...] = turned[:pairs, :share]
+    spec_ref[...] = turned[:, :share]
 
     with jax.named_scope("drain"):
-        whole(harm_v, harm_sem).wait()
         whole(send0, sent_sems.at[0]).wait()
         whole(coef_send, sent_sems.at[1]).wait()
         for s in range(steps):
@@ -446,38 +445,24 @@
     whole(pow_v.at[: tiles - 1], sent_sems.at[2 + steps]).wait()
 
 
-def hand_over_body(parts, large_ref, small_ref, large_out, small_out, large_v, small_v, sems, small_sems):
-    rows = large_v.shape[0] // parts
-    ins, outs = [], []
-    for c in range(parts):
-        picked = slice(c * rows, (c + 1) * rows)
-        ins.append(pltpu.make_async_copy(large_ref.at[picked], large_v.at[picked], sems.at[0, c]))
-        outs.append(pltpu.make_async_copy(large_v.at[picked], large_out.at[picked], sems.at[1, c]))
-    ins.append(pltpu.make_async_copy(small_ref, small_v, small_sems.at[0]))
-    outs.append(pltpu.make_async_copy(small_v, small_out, small_sems.at[1]))
-    for copy in ins:
+def hand_over_body(large_ref, small_ref, large_out, small_out, sems):
+    copies = [
+        pltpu.make_async_copy(large_ref, large_out, sems.at[0]),
+        pltpu.make_async_copy(small_ref, small_out, sems.at[1]),
+    ]
+    for copy in copies:
         copy.start()
-    for got, put in zip(ins, outs):
-        got.wait()
-        put.start()
-    for copy in outs:
+    for copy in copies:
         copy.wait()
 
 
 def hand_over(large, small):
-    parts = 4
-    anywhere = pl.BlockSpec(memory_space=pl.ANY)
     return pl.pallas_call(
-        functools.partial(hand_over_body, parts),
+        hand_over_body,
         out_shape=[jax.ShapeDtypeStruct(large.shape, large.dtype), jax.ShapeDtypeStruct(small.shape, small.dtype)],
-        in_specs=[anywhere] * 2,
-        out_specs=[anywhere] * 2,
-        scratch_shapes=[
-            pltpu.VMEM(large.shape, large.dtype),
-            pltpu.VMEM(small.shape, small.dtype),
-            pltpu.SemaphoreType.DMA((2, parts)),
-            pltpu.SemaphoreType.DMA((2,)),
-        ],
+        in_specs=[pl.BlockSpec(memory_space=pltpu.VMEM)] * 2,
+        out_specs=[pl.BlockSpec(memory_space=pl.ANY)] * 2,
+        scratch_shapes=[pltpu.SemaphoreType.DMA((2,))],
         cost_estimate=pl.CostEstimate(flops=large.size, bytes_accessed=8 * large.size, transcendentals=0),
     )(large, small)
 
@@ -499,7 +484,6 @@
     tiles = ells // tile
     sharers = tile * devices // ells
     pairs = maps * (maps + 1) // 2
-    padded = -(-pairs // 8) * 8
     first, high, low = fourier_tables(pixels, orders, tile)
     rows0 = block * channels
     halves = []
@@ -507,6 +491,8 @@
         halves += [pltpu.VMEM((2, chunks, rows0 >> (s + 1), width), BF16)] * 2
     cfg = (maps, cycles, orders, ells, devices, grp, width)
     scratch = [
+        pltpu.SMEM((orders,), jnp.int32),
+        pltpu.VMEM((1, orders), jnp.int32),
         pltpu.VMEM((chunks, cycles, orders, width), BF16),
         pltpu.VMEM((maps, cycles, coarse, tile), F32),
         pltpu.VMEM(first.shape, F32),
@@ -522,19 +508,17 @@
         pltpu.VMEM((2, 3, block, tile), BF16),
         pltpu.VMEM((2, chunks, rows0 // 2, width), F32),
         halves,
-        pltpu.VMEM((chunks, own * maps, 2, width), F32),
-        pltpu.VMEM((tiles, padded, tile), F32),
-        pltpu.VMEM((tiles, padded, tile), F32),
-        pltpu.VMEM((padded, tile), F32),
-        pltpu.VMEM((sharers - 1, padded, tile), F32),
+        pltpu.VMEM((tiles, pairs, tile), F32),
+        pltpu.VMEM((tiles, pairs, tile), F32),
+        pltpu.VMEM((pairs, tile), F32),
+        pltpu.VMEM((sharers - 1, pairs, tile), F32),
         pltpu.SemaphoreType.DMA((4,)),
         pltpu.SemaphoreType.DMA,
-        pltpu.SemaphoreType.DMA((3,)),
+        pltpu.SemaphoreType.DMA((5,)),
         pltpu.SemaphoreType.DMA((3 + steps,)),
         pltpu.SemaphoreType.DMA((SLOTS, 2)),
         pltpu.SemaphoreType.DMA((2,)),
         pltpu.SemaphoreType.DMA((steps, SLOTS, 2)),
-        pltpu.SemaphoreType.DMA,
         pltpu.SemaphoreType.DMA,
         pltpu.SemaphoreType.DMA((2, sharers - 1)),
     ]
@@ -543,14 +527,14 @@
     harmonics, spectra = pl.pallas_call(
         functools.partial(kernel, cfg),
         out_shape=[
-            jax.ShapeDtypeStruct((own * maps, 2, ells), F32),
-            jax.ShapeDtypeStruct((pairs, ells // devices), F32),
+            pltpu.VMEM((own * maps, 2, ells), F32),
+            pltpu.VMEM((pairs, ells // devices), F32),
         ],
-        in_specs=[pl.BlockSpec(memory_space=pltpu.SMEM), vmem] + [anywhere] * 5,
-        out_specs=[anywhere, vmem],
+        in_specs=[anywhere] * 7,
+        out_specs=[vmem, vmem],
         scratch_shapes=scratch,
         compiler_params=pltpu.CompilerParams(
-            vmem_limit_bytes=60 * MIB, collective_id=0, has_side_effects=True
+            vmem_limit_bytes=56 * MIB, collective_id=0, has_side_effects=True
         ),
         cost_estimate=pl.CostEstimate(
             flops=2 * cycles * orders * orders * ells, bytes_accessed=2 * legendre.size, transcendentals=0
@@ -564,6 +548,7 @@
         jnp.asarray(low),
         legendre,
     )
+    harmonics, spectra = (pltpu.with_memory_space_constraint(v, pltpu.VMEM) for v in (harmonics, spectra))
     harmonics, spectra = hand_over(harmonics, spectra)
     return harmonics.reshape(own, maps, 2, ells), spectra
 

time: 81.7 us -> 77.4 us (0.947)
  Pallas kernels: 80.4 us -> 76.6 us
    pallas_call x2, Pallas kernels: 80.4 us -> 76.6 us  [the longest x1 75.6 us: per_device(): pl.pallas_call(functools.partial(kernel, cfg), out_shape=[pltpu.VMEM((own...]
where the time goes in v3:
time: 77.4 us; the launch traced here: 77.3 us
  Pallas kernels  76.6 us (99%)
    pallas_call x1, Pallas kernels, per_device(): pl.pallas_call(functools.partial(kernel, cfg), out_shape=[pltpu.VMEM((own...  75.6 us

profile of v3, /device:TPU:31, one launch (start us, length us, event | category | flops | bytes accessed | tf_op | source)
XLA Modules:
  0.0 77.3 jit_solution(7195114559517681355)
XLA Ops:
  0.6 75.6 %shard_map.77 = (f32[64,2,2048]{2,1,0:T(2,128)S(1)}, f32[10,64]{1,0:T(8,128)S(1)}) custom-call(s32[512]{0:T(512)} %owner_hbm.1, s32[1,512]{1,0:T(1,128)} %bitcast.3, f32[4,4,4096]{2,1,0:T(4,128)} %sky_hbm.1, f32[64,32]{1,0:T(8,128)} %constant.6.clone.first_hbm, bf16[256,1024]{1,0:T(8,128)(2,1)} %constant.7.clone.high_hbm, ...), custom_call_target="tpu_custom_call" | custom-call | flops 4294967296 | bytes 8388608 | tf_op jit(solution)/shard_map/pallas_call | solution.py:527
  76.3 1.0 %shard_map.78 = (f32[64,2,2048]{2,1,0:T(2,128)}, f32[10,64]{1,0:T(8,128)}) custom-call(f32[64,2,2048]{2,1,0:T(2,128)S(1)} %get-tuple-element.6.large_ref, f32[10,64]{1,0:T(8,128)S(1)} %get-tuple-element.7.small_ref), custom_call_target="tpu_custom_call" | custom-call | flops 262144 | bytes 2097152 | tf_op jit(solution)/shard_map/pallas_call | solution.py:460

commit v4 on v3

--- a/solution.py
+++ b/solution.py
@@ -19,6 +19,7 @@
 EARLY = 3
 WIDTH = 128
 AHEAD = 3
+CROSS = 1
 SWAPPED = 2
 SLOTS = 8
 LAGS = (2, 2, 3)
@@ -93,8 +94,14 @@
     def bit(b):
         return (me // (1 << b)) % 2
 
-    gather = [[None, flip(me, [0]), flip(me, [FIRST[ty]]), flip(me, [FIRST[ty], 0])] for ty in range(2)]
-    near = sorted({(0,)} | {(f,) for f in FIRST} | {(0, f) for f in FIRST} | {(b,) for b in range(1, bits)})
+    gather = [
+        [[None, flip(me, [0]), flip(me, [b]), flip(me, [b, 0])] for b in firsts] for firsts in (FIRST, (EARLY, EARLY))
+    ]
+    near = sorted({(b,) for b in range(bits)} | {(0, b) for b in FIRST + (EARLY,)})
+
+    def group_row(variant, p, g):
+        q = p * 4 + g if variant == 0 else (g // 2) * 8 + (p % 2) * 4 + (p // 2) * 2 + g % 2
+        return q * GROUP
 
     scope = jax.named_scope
     row_load = pltpu.make_async_copy(owner_row_hbm, owner_ref, table_sem.at[3])
@@ -155,23 +162,23 @@
     def whole(ref, sem):
         return pltpu.make_async_copy(ref, ref, sem)
 
-    def gather_copy(ty, t, p):
+    def gather_copy(ty, t, p, variant):
         return pltpu.make_async_remote_copy(
             src_ref=send0.at[ty, t, p - 1],
             dst_ref=recv0.at[ty, t, p - 1],
             send_sem=sent_sems.at[0],
             recv_sem=sems0.at[t % SLOTS, ty],
-            device_id=at(gather[ty][p]),
+            device_id=at(gather[variant][ty][p]),
             device_id_type=MESH,
         )
 
-    def coef_copy(ty, p):
+    def coef_copy(variant, ty, p):
         return pltpu.make_async_remote_copy(
-            src_ref=coef_send.at[ty, p - 1],
-            dst_ref=coef_recv.at[ty, p - 1],
+            src_ref=coef_send.at[variant, ty, p - 1],
+            dst_ref=coef_recv.at[variant, ty, p - 1],
             send_sem=sent_sems.at[1],
-            recv_sem=coef_sems.at[ty],
-            device_id=at(gather[ty][p]),
+            recv_sem=coef_sems.at[variant, ty],
+            device_id=at(gather[variant][ty][p]),
             device_id_type=MESH,
         )
 
@@ -182,6 +189,8 @@
         partner = flip(me, [later[ty][s]])
         if s < 2:
             partner = jnp.where(t < swap_from, partner, flip(me, [later[ty][1 - s]]))
+        if s == 0:
+            partner = jnp.where(t == CROSS, flip(me, [FIRST[ty]]), partner)
         return pltpu.make_async_remote_copy(
             src_ref=halves[2 * s].at[ty, t],
             dst_ref=halves[2 * s + 1].at[ty, t],
@@ -191,17 +200,17 @@
             device_id_type=MESH,
         )
 
-    def permute(t):
+    def permute(t, variant=0):
         with jax.named_scope("load"):
             load(t).wait()
         with jax.named_scope("permute"):
-            permute_loaded(t)
+            permute_loaded(t, variant)
 
         @pl.when(t + 4 < chunks)
         def _():
             load(t + 4).start()
 
-    def permute_loaded(t):
+    def permute_loaded(t, variant):
         together = max(1, 256 // width)
         for r0 in range(0, cycles, together):
             values = jnp.concatenate([leg_v[t, r0 + i] for i in range(together)], axis=1)
@@ -209,16 +218,21 @@
                 picked = dot(hot_v[ty * 4 * block : (ty + 1) * 4 * block, :], values).astype(BF16)
                 for i in range(together):
                     piece = picked[:, i * width : (i + 1) * width]
-                    own0[ty, t, r0 + i] = piece[:block]
-                    for p in range(1, 4):
-                        send0[ty, t, p - 1, r0 + i] = piece[p * block : (p + 1) * block]
+                    for p in range(4):
+                        rows = [group_row(variant, p, g) for g in range(groups)]
+                        rows = jnp.concatenate([piece[row : row + GROUP] for row in rows], axis=0)
+                        if p == 0:
+                            own0[ty, t, r0 + i] = rows
+                        else:
+                            send0[ty, t, p - 1, r0 + i] = rows
         for p in (2, 3, 1):
             for ty in range(2):
-                gather_copy(ty, t, p).start()
+                gather_copy(ty, t, p, variant).start()
 
     with jax.named_scope("barrier"):
         pl.semaphore_wait(barrier, len(near))
     permute(0)
+    permute(CROSS, 1)
     order_load = pltpu.make_async_copy(owner_hbm, owner_smem, table_sem.at[4])
     order_load.start()
 
@@ -248,16 +262,25 @@
     spectral = jnp.concatenate(
         [jnp.concatenate(spectral[:2], axis=1), jnp.concatenate(spectral[2:], axis=1)], axis=0
     ).astype(BF16)
-    spectral = jnp.concatenate([spectral, jnp.zeros((tile - 2 * count, orders), BF16)], axis=0)
-    coef = dot_t(hot_v[...], spectral).astype(BF16)
-    for ty in range(2):
-        base = ty * 4 * block
-        coef_own[ty] = coef[base : base + block]
-        for p in range(1, 4):
-            coef_send[ty, p - 1] = coef[base + p * block : base + (p + 1) * block]
-    for p in (2, 3, 1):
+    copies = tile // (2 * count)
+    coef = dot_t(hot_v[...], jnp.concatenate([spectral] * copies, axis=0))
+    lane_group = lax.broadcasted_iota(jnp.int32, (GROUP, tile), 1) // (2 * count)
+    for variant in range(2):
         for ty in range(2):
-            coef_copy(ty, p).start()
+            for p in range(4):
+                packed = None
+                for g in range(groups):
+                    row = ty * 4 * block + group_row(variant, p, g)
+                    rows = coef[row : row + GROUP]
+                    packed = rows if packed is None else jnp.where(lane_group == g, rows, packed)
+                if p == 0:
+                    coef_own[variant, ty] = packed.astype(BF16)
+                else:
+                    coef_send[variant, ty, p - 1] = packed.astype(BF16)
+    for variant in range(2):
+        for p in (2, 3, 1):
+            for ty in range(2):
+                coef_copy(variant, ty, p).start()
 
     order_load.wait()
 
@@ -265,51 +288,54 @@
         permute(t)
         return carry
 
-    lax.fori_loop(1, AHEAD + 1, permute_step, 0)
+    lax.fori_loop(CROSS + 1, AHEAD + 1, permute_step, 0)
 
     source = lax.broadcasted_iota(jnp.int32, (tile, cycles * tile), 0)
     target = lax.broadcasted_iota(jnp.int32, (tile, cycles * tile), 1)
-    channel = 2 * ((source // cycles) % maps) + source // count
-    same = (source % cycles == target // tile) & (channel == target % channels) & (source < 2 * count)
+    channel = 2 * ((source // cycles) % maps) + (source // count) % 2
+    same = (source % cycles == target // tile) & (channel == target % channels)
     expand = jnp.where(same, 1.0, 0.0).astype(BF16)
     depth = 4 * cycles * GROUP
     keep = lax.broadcasted_iota(jnp.int32, (depth, tile), 0) % GROUP == (
         lax.broadcasted_iota(jnp.int32, (depth, tile), 1) // channels
     )
-    for ty in range(2):
-        spread = []
-        with jax.named_scope("waitcoef"):
-            whole(coef_recv.at[ty], coef_sems.at[ty]).wait()
-        for p in range(4):
-            values = coef_recv[ty, p - 1] if p else coef_own[ty]
-            spread.append(dot(values, expand))
-        for g in range(block // GROUP):
-            pieces = [
-                spread[p][g * GROUP : (g + 1) * GROUP, r * tile : (r + 1) * tile]
-                for p in range(4)
-                for r in range(cycles)
-            ]
-            stacked = jnp.where(keep, jnp.concatenate(pieces, axis=0), 0.0)
-            lhs_v[ty, g] = stacked.T.astype(BF16)
-
+    pack_group = lax.broadcasted_iota(jnp.int32, (4 * GROUP, tile), 1) // (2 * count)
+
+    def build(variant):
+        for ty in range(2):
+            with scope("waitcoef"):
+                whole(coef_recv.at[variant, ty], coef_sems.at[variant, ty]).wait()
+            values = [coef_own[variant, ty]] + [coef_recv[variant, ty, p] for p in range(3)]
+            values = jnp.concatenate(values, axis=0).astype(F32)
+            for g in range(groups):
+                spread = dot(jnp.where(pack_group == g, values, 0.0).astype(BF16), expand)
+                pieces = [
+                    spread[p * GROUP : (p + 1) * GROUP, r * tile : (r + 1) * tile]
+                    for p in range(4)
+                    for r in range(cycles)
+                ]
+                stacked = jnp.where(keep, jnp.concatenate(pieces, axis=0), 0.0)
+                lhs_v[variant, ty, g] = stacked.T.astype(BF16)
+
+    build(0)
     high_rows = GROUP * channels
 
-    def product(ty, t, g):
+    def product(variant, ty, t, g):
         span = slice(g * GROUP, (g + 1) * GROUP)
         parts = [own0[ty, t, :, span, :]] + [recv0[ty, t, p, :, span, :] for p in range(3)]
         right = jnp.concatenate([v.reshape(cycles * GROUP, width) for v in parts], axis=0)
-        return dot(lhs_v[ty, g], right)
-
-    def first_step(t, sent, kept):
+        return dot(lhs_v[variant, ty, g], right)
+
+    def first_step(t, sent, kept, variant=0):
         for ty in range(2):
             with jax.named_scope("wait0"):
                 whole(recv0.at[ty, t], sems0.at[t % SLOTS, ty]).wait()
             for i, g in enumerate(sent):
-                halves[0][ty, t, i * high_rows : (i + 1) * high_rows, :] = product(ty, t, g).astype(BF16)
+                halves[0][ty, t, i * high_rows : (i + 1) * high_rows, :] = product(variant, ty, t, g).astype(BF16)
             half_copy(0, ty, t).start()
         for ty in range(2):
             for i, g in enumerate(kept):
-                acc_v[ty, t, i * high_rows : (i + 1) * high_rows, :] = product(ty, t, g)
+                acc_v[ty, t, i * high_rows : (i + 1) * high_rows, :] = product(variant, ty, t, g)
 
     def next_step(s, t):
         size = rows0 >> (s + 1)
@@ -376,10 +402,17 @@
         def _():
             permute(t + AHEAD)
 
-        @pl.when(t < swap_from)
+        @pl.when((t < swap_from) & (t != CROSS))
         def _():
             with jax.named_scope("first"):
                 first_step(t, (2, 3), (0, 1))
+
+        @pl.when(t == CROSS)
+        def _():
+            with jax.named_scope("build"):
+                build(1)
+            with jax.named_scope("first"):
+                first_step(t, (2, 3), (0, 1), 1)
 
         @pl.when((t >= swap_from) & (t < chunks))
         def _():
@@ -499,13 +532,13 @@
         pltpu.VMEM(high.shape, BF16),
         pltpu.VMEM(low.shape, BF16),
         pltpu.VMEM((orders, orders), BF16),
-        pltpu.VMEM((2, block // GROUP, GROUP * channels, 4 * cycles * GROUP), BF16),
+        pltpu.VMEM((2, 2, block // GROUP, GROUP * channels, 4 * cycles * GROUP), BF16),
         pltpu.VMEM((2, chunks, cycles, block, width), BF16),
         pltpu.VMEM((2, chunks, 3, cycles, block, width), BF16),
         pltpu.VMEM((2, chunks, 3, cycles, block, width), BF16),
-        pltpu.VMEM((2, block, tile), BF16),
-        pltpu.VMEM((2, 3, block, tile), BF16),
-        pltpu.VMEM((2, 3, block, tile), BF16),
+        pltpu.VMEM((2, 2, GROUP, tile), BF16),
+        pltpu.VMEM((2, 2, 3, GROUP, tile), BF16),
+        pltpu.VMEM((2, 2, 3, GROUP, tile), BF16),
         pltpu.VMEM((2, chunks, rows0 // 2, width), F32),
         halves,
         pltpu.VMEM((tiles, pairs, tile), F32),
@@ -517,7 +550,7 @@
         pltpu.SemaphoreType.DMA((5,)),
         pltpu.SemaphoreType.DMA((3 + steps,)),
         pltpu.SemaphoreType.DMA((SLOTS, 2)),
-        pltpu.SemaphoreType.DMA((2,)),
+        pltpu.SemaphoreType.DMA((2, 2)),
         pltpu.SemaphoreType.DMA((steps, SLOTS, 2)),
         pltpu.SemaphoreType.DMA,
         pltpu.SemaphoreType.DMA((2, sharers - 1)),

time: 77.4 us -> 75.3 us (0.973)
  Pallas kernels: 76.6 us -> 74.5 us
    pallas_call x1, Pallas kernels: 75.6 us -> 73.5 us  [per_device(): pl.pallas_call(functools.partial(kernel, cfg), out_shape=[pltpu.VMEM((own...]
where the time goes in v4:
time: 75.3 us; the launch traced here: 75.2 us
  Pallas kernels  74.5 us (99%)
    pallas_call x1, Pallas kernels, per_device(): pl.pallas_call(functools.partial(kernel, cfg), out_shape=[pltpu.VMEM((own...  73.5 us

profile of v4, /device:TPU:31, one launch (start us, length us, event | category | flops | bytes accessed | tf_op | source)
XLA Modules:
  0.0 75.2 jit_solution(3451249670944323211)
XLA Ops:
  0.6 73.5 %shard_map.77 = (f32[64,2,2048]{2,1,0:T(2,128)S(1)}, f32[10,64]{1,0:T(8,128)S(1)}) custom-call(s32[512]{0:T(512)} %owner_hbm.1, s32[1,512]{1,0:T(1,128)} %bitcast.3, f32[4,4,4096]{2,1,0:T(4,128)} %sky_hbm.1, f32[64,32]{1,0:T(8,128)} %constant.6.clone.first_hbm, bf16[256,1024]{1,0:T(8,128)(2,1)} %constant.7.clone.high_hbm, ...), custom_call_target="tpu_custom_call" | custom-call | flops 4294967296 | bytes 8388608 | tf_op jit(solution)/shard_map/pallas_call | solution.py:560
  74.2 1.0 %shard_map.78 = (f32[64,2,2048]{2,1,0:T(2,128)}, f32[10,64]{1,0:T(8,128)}) custom-call(f32[64,2,2048]{2,1,0:T(2,128)S(1)} %get-tuple-element.6.large_ref, f32[10,64]{1,0:T(8,128)S(1)} %get-tuple-element.7.small_ref), custom_call_target="tpu_custom_call" | custom-call | flops 262144 | bytes 2097152 | tf_op jit(solution)/shard_map/pallas_call | solution.py:493

commit v5 on v4

--- a/solution.py
+++ b/solution.py
@@ -20,7 +20,12 @@
 WIDTH = 128
 AHEAD = 3
 CROSS = 1
-SWAPPED = 2
+SWAPPED = 1
+FINALE = (
+    *((1, 4), (0, 2), (3, 9), (3, 8), (1, 3), (0, 1), (2, 6), (2, 5), (3, 7), (2, 4), (2, 3)),
+    *((1, 2), (1, 1), (3, 6), (2, 2), (3, 5), (2, 1), (3, 4), (3, 3), (3, 2), (3, 1)),
+)
+ROTATE = 0
 SLOTS = 8
 LAGS = (2, 2, 3)
 
@@ -68,7 +73,7 @@
 
 def kernel(
     cfg, owner_hbm, owner_row_hbm, sky_hbm, first_hbm, high_hbm, low_hbm, leg_hbm, harm_ref, spec_ref,
-    owner_smem, owner_ref, leg_v, sky_v, first_v, high_v, low_v, hot_v, lhs_v, own0, send0, recv0, coef_own, coef_send, coef_recv,
+    owner_smem, owner_ref, column_v, leg_v, sky_v, first_v, high_v, low_v, hot_v, lhs_v, own0, send0, recv0, coef_own, coef_send, coef_recv,
     acc_v, halves, pow_v, pow_recv, pow_mine, pow_pair, load_sem, sky_sem, table_sem,
     sent_sems, sems0, coef_sems, half_sems, pow_sem, pair_sems,
 ):
@@ -97,7 +102,7 @@
     gather = [
         [[None, flip(me, [0]), flip(me, [b]), flip(me, [b, 0])] for b in firsts] for firsts in (FIRST, (EARLY, EARLY))
     ]
-    near = sorted({(b,) for b in range(bits)} | {(0, b) for b in FIRST + (EARLY,)})
+    near = sorted({(b,) for b in range(bits)} | {(0, b) for b in FIRST + (EARLY,)}, reverse=True)
 
     def group_row(variant, p, g):
         q = p * 4 + g if variant == 0 else (g // 2) * 8 + (p % 2) * 4 + (p // 2) * 2 + g % 2
@@ -110,8 +115,11 @@
     for masks in near:
         pl.semaphore_signal(barrier, inc=1, device_id=at(flip(me, masks)), device_id_type=MESH)
 
+    def place_of(t):
+        return (t + ROTATE * chunks // 16) % chunks
+
     def load(t):
-        lanes = pl.ds(pl.multiple_of(t * width, width), width)
+        lanes = pl.ds(pl.multiple_of(place_of(t) * width, width), width)
         return pltpu.make_async_copy(leg_hbm.at[:, :, lanes], leg_v.at[t], load_sem.at[t % 4])
 
     def load_start(t, carry):
@@ -136,28 +144,47 @@
         table.start()
 
 
-    j = lax.broadcasted_iota(jnp.int32, (orders, tile), 0)
     half_bit, block_bit = (orders // 2).bit_length() - 1, block.bit_length() - 1
-    part = j >> half_bit
-    slot = part * per_type + (j & (per_type - 1))
 
     def place(b, differs):
         mine = bit(b)
         return (mine + differs - 2 * mine * differs) * ((1 << b) * own)
 
-    slot = slot + place(0, (j >> block_bit) & 1)
-    for ty in range(2):
-        terms = place(FIRST[ty], (j >> (block_bit + 1)) & 1)
-        for s, b in enumerate(later[ty]):
-            terms = terms + place(b, (j >> (block_bit - s - 1)) & 1)
-        slot = slot + jnp.where(part == ty, terms, 0)
     lane = lax.broadcasted_iota(jnp.int32, (orders, tile), 1)
-    pick = jnp.concatenate(
-        [jnp.where(slot == lane + c * tile, 1.0, 0.0).astype(BF16) for c in range(orders // tile)], axis=1
-    )
-    row_load.wait()
-    table = jnp.where(lax.broadcasted_iota(jnp.int32, (orders, orders), 0) == owner_ref[...], 1.0, 0.0).astype(BF16)
-    hot_v[...] = dot_t(pick, table).astype(BF16)
+    if per_type % 8 == 0:
+        places = [[place(b, differs) for differs in range(2)] for b in range(bits)]
+        row_load.wait()
+        for c in range(orders // tile):
+            row = owner_ref[:, c * tile : (c + 1) * tile].astype(F32)
+            column_v[c * tile : (c + 1) * tile, :] = jnp.broadcast_to(row, (tile, tile)).T
+        picked = []
+        for jb in range(0, orders, 8):
+            ty = jb >> half_bit
+            start = ty * per_type + jb % per_type + places[0][(jb >> block_bit) & 1]
+            start = start + places[FIRST[ty]][(jb >> (block_bit + 1)) & 1]
+            for s, b in enumerate(later[ty]):
+                start = start + places[b][(jb >> (block_bit - s - 1)) & 1]
+            picked.append(column_v[pl.ds(pl.multiple_of(start, 8), 8), :])
+        column = jnp.concatenate(picked, axis=0)
+        lane = lane.astype(F32)
+        for c in range(orders // tile):
+            hot_v[:, c * tile : (c + 1) * tile] = jnp.where(column == lane + float(c * tile), 1.0, 0.0).astype(BF16)
+    else:
+        j = lax.broadcasted_iota(jnp.int32, (orders, tile), 0)
+        part = j >> half_bit
+        slot = part * per_type + (j & (per_type - 1)) + place(0, (j >> block_bit) & 1)
+        for ty in range(2):
+            terms = place(FIRST[ty], (j >> (block_bit + 1)) & 1)
+            for s, b in enumerate(later[ty]):
+                terms = terms + place(b, (j >> (block_bit - s - 1)) & 1)
+            slot = slot + jnp.where(part == ty, terms, 0)
+        pick = jnp.concatenate(
+            [jnp.where(slot == lane + c * tile, 1.0, 0.0).astype(BF16) for c in range(orders // tile)], axis=1
+        )
+        row_load.wait()
+        index = lax.broadcasted_iota(jnp.int32, (orders, orders), 0)
+        table = jnp.where(index == owner_ref[...], 1.0, 0.0).astype(BF16)
+        hot_v[...] = dot_t(pick, table).astype(BF16)
 
     def whole(ref, sem):
         return pltpu.make_async_copy(ref, ref, sem)
@@ -200,11 +227,20 @@
             device_id_type=MESH,
         )
 
-    def permute(t, variant=0):
+    def enter():
+        with jax.named_scope("barrier"):
+            pl.semaphore_wait(barrier, len(near))
+
+    def permute(t, variant=0, entered=False):
         with jax.named_scope("load"):
             load(t).wait()
         with jax.named_scope("permute"):
             permute_loaded(t, variant)
+        if entered:
+            enter()
+        for p in (2, 3, 1):
+            for ty in range(2):
+                gather_copy(ty, t, p, variant).start()
 
         @pl.when(t + 4 < chunks)
         def _():
@@ -225,13 +261,8 @@
                             own0[ty, t, r0 + i] = rows
                         else:
                             send0[ty, t, p - 1, r0 + i] = rows
-        for p in (2, 3, 1):
-            for ty in range(2):
-                gather_copy(ty, t, p, variant).start()
-
-    with jax.named_scope("barrier"):
-        pl.semaphore_wait(barrier, len(near))
-    permute(0)
+
+    permute(0, entered=True)
     permute(CROSS, 1)
     order_load = pltpu.make_async_copy(owner_hbm, owner_smem, table_sem.at[4])
     order_load.start()
@@ -360,9 +391,9 @@
 
     def last_step(t):
         size = rows0 >> steps
-        ell = t * width + lax.broadcasted_iota(jnp.int32, (channels, width), 1)
+        ell = place_of(t) * width + lax.broadcasted_iota(jnp.int32, (channels, width), 1)
         total = [None] * (maps // 2 + 1)
-        lanes = pl.ds(pl.multiple_of(t * width, width), width)
+        lanes = pl.ds(pl.multiple_of(place_of(t) * width, width), width)
         for ty in range(2):
             with jax.named_scope("waitlast"):
                 half_copy(steps - 1, ty, t).wait_recv()
@@ -385,7 +416,7 @@
                 rows.append(total[k][2 * a : 2 * a + 1] + total[k][2 * a + 1 : 2 * a + 2])
         power = jnp.concatenate(rows, axis=0)
         for h in range(width // tile):
-            u = t * (width // tile) + h
+            u = place_of(t) * (width // tile) + h
             pow_v[u] = power[:, h * tile : (h + 1) * tile]
 
             @pl.when(u != me // sharers)
@@ -397,43 +428,59 @@
         lags.append(lags[-1] + LAGS[1])
     end = lags[-1] + LAGS[2]
 
+    def first_of(t):
+        @pl.when((t < swap_from) & (t != CROSS))
+        def _():
+            with scope("first"):
+                first_step(t, (2, 3), (0, 1))
+
+        @pl.when(t == CROSS)
+        def _():
+            with scope("build"):
+                build(1)
+            with scope("first"):
+                first_step(t, (2, 3), (0, 1), 1)
+
+        @pl.when((t >= swap_from) & (t < chunks))
+        def _():
+            with scope("first"):
+                first_step(t, (1, 3), (0, 2))
+
+    def later_of(t):
+        for s in range(1, steps):
+
+            @pl.when((t >= lags[s]) & (t < chunks + lags[s]))
+            def _():
+                with scope(f"next{s}"):
+                    next_step(s, t - lags[s])
+
+        @pl.when(t >= end)
+        def _():
+            with scope("last"):
+                last_step(t - end)
+
     def main(t, carry):
         @pl.when((t > 0) & (t + AHEAD < chunks))
         def _():
             permute(t + AHEAD)
 
-        @pl.when((t < swap_from) & (t != CROSS))
-        def _():
-            with jax.named_scope("first"):
-                first_step(t, (2, 3), (0, 1))
-
-        @pl.when(t == CROSS)
-        def _():
-            with jax.named_scope("build"):
-                build(1)
-            with jax.named_scope("first"):
-                first_step(t, (2, 3), (0, 1), 1)
-
-        @pl.when((t >= swap_from) & (t < chunks))
-        def _():
-            with jax.named_scope("first"):
-                first_step(t, (1, 3), (0, 2))
-
-        for s in range(1, steps):
-
-            @pl.when((t >= lags[s]) & (t < chunks + lags[s]))
-            def _():
-                with jax.named_scope(f"next{s}"):
-                    next_step(s, t - lags[s])
-
-        @pl.when(t >= end)
-        def _():
-            with jax.named_scope("last"):
-                last_step(t - end)
-
+        first_of(t)
+        later_of(t)
         return carry
 
-    lax.fori_loop(0, chunks + end, main, 0)
+    special = steps == 3 and chunks >= 14
+    lax.fori_loop(0, chunks - 2 if special else chunks + end, main, 0)
+    if special:
+        with scope("finale"):
+            for e, back in FINALE:
+                t = chunks - back
+                with scope(f"e{e}"):
+                    if e == 0:
+                        first_step(t, (1, 3) if back <= SWAPPED else (2, 3), (0, 2) if back <= SWAPPED else (0, 1))
+                    elif e < 3:
+                        next_step(e, t)
+                    else:
+                        last_step(t)
 
     mine = me // sharers
     total = pow_v[mine]
@@ -526,6 +573,7 @@
     scratch = [
         pltpu.SMEM((orders,), jnp.int32),
         pltpu.VMEM((1, orders), jnp.int32),
+        pltpu.VMEM((orders, tile), F32),
         pltpu.VMEM((chunks, cycles, orders, width), BF16),
         pltpu.VMEM((maps, cycles, coarse, tile), F32),
         pltpu.VMEM(first.shape, F32),

time: 75.3 us -> 74.9 us (level)
  no operation moved by 1% of the time
where the time goes in v5:
time: 74.9 us; the launch traced here: 74.7 us
  Pallas kernels  74.1 us (99%)
    pallas_call x1, Pallas kernels, per_device(): pl.pallas_call(functools.partial(kernel, cfg), out_shape=[pltpu.VMEM((own...  73.1 us

profile of v5, /device:TPU:31, one launch (start us, length us, event | category | flops | bytes accessed | tf_op | source)
XLA Modules:
  0.0 74.7 jit_solution(14667631014279827494)
XLA Ops:
  0.6 73.1 %shard_map.77 = (f32[64,2,2048]{2,1,0:T(2,128)S(1)}, f32[10,64]{1,0:T(8,128)S(1)}) custom-call(s32[512]{0:T(512)} %owner_hbm.1, s32[1,512]{1,0:T(1,128)} %bitcast.3, f32[4,4,4096]{2,1,0:T(4,128)} %sky_hbm.1, f32[64,32]{1,0:T(8,128)} %constant.6.clone.first_hbm, bf16[256,1024]{1,0:T(8,128)(2,1)} %constant.7.clone.high_hbm, ...), custom_call_target="tpu_custom_call" | custom-call | flops 4294967296 | bytes 8388608 | tf_op jit(solution)/shard_map/pallas_call | solution.py:608
  73.7 1.0 %shard_map.78 = (f32[64,2,2048]{2,1,0:T(2,128)}, f32[10,64]{1,0:T(8,128)}) custom-call(f32[64,2,2048]{2,1,0:T(2,128)S(1)} %get-tuple-element.6.large_ref, f32[10,64]{1,0:T(8,128)S(1)} %get-tuple-element.7.small_ref), custom_call_target="tpu_custom_call" | custom-call | flops 262144 | bytes 2097152 | tf_op jit(solution)/shard_map/pallas_call | solution.py:540

commit v6 on v5

--- a/solution.py
+++ b/solution.py
@@ -74,8 +74,8 @@
 def kernel(
     cfg, owner_hbm, owner_row_hbm, sky_hbm, first_hbm, high_hbm, low_hbm, leg_hbm, harm_ref, spec_ref,
     owner_smem, owner_ref, column_v, leg_v, sky_v, first_v, high_v, low_v, hot_v, lhs_v, own0, send0, recv0, coef_own, coef_send, coef_recv,
-    acc_v, halves, pow_v, pow_recv, pow_mine, pow_pair, load_sem, sky_sem, table_sem,
-    sent_sems, sems0, coef_sems, half_sems, pow_sem, pair_sems,
+    acc_v, halves, pow_v, pow_recv, pow_mine, pow_pair, pow_total, pow_direct, load_sem, sky_sem, table_sem,
+    sent_sems, sems0, coef_sems, half_sems, pow_sems, pair_sems,
 ):
     maps, cycles, orders, ells, devices, grp, width = cfg
     bits = devices.bit_length() - 1
@@ -384,12 +384,22 @@
             src_ref=pow_v.at[u],
             dst_ref=pow_recv.at[me // sharers],
             send_sem=sent_sems.at[2 + steps],
-            recv_sem=pow_sem,
+            recv_sem=pow_sems.at[0],
             device_id=at(u * sharers + me % sharers),
             device_id_type=MESH,
         )
 
-    def last_step(t):
+    def direct_copy(u, owner):
+        return pltpu.make_async_remote_copy(
+            src_ref=pow_v.at[u],
+            dst_ref=pow_direct.at[me],
+            send_sem=sent_sems.at[3 + steps],
+            recv_sem=pow_sems.at[1],
+            device_id=at(owner),
+            device_id_type=MESH,
+        )
+
+    def last_step(t, direct=False):
         size = rows0 >> steps
         ell = place_of(t) * width + lax.broadcasted_iota(jnp.int32, (channels, width), 1)
         total = [None] * (maps // 2 + 1)
@@ -419,9 +429,18 @@
             u = place_of(t) * (width // tile) + h
             pow_v[u] = power[:, h * tile : (h + 1) * tile]
 
-            @pl.when(u != me // sharers)
-            def _():
-                pow_copy(u).start()
+            if direct:
+                for e in range(sharers):
+
+                    @pl.when(u * sharers + e != me)
+                    def _():
+                        direct_copy(u, u * sharers + e).start()
+
+            else:
+
+                @pl.when(u != me // sharers)
+                def _():
+                    pow_copy(u).start()
 
     lags = [0, LAGS[0]]
     for s in range(2, steps):
@@ -480,15 +499,10 @@
                     elif e < 3:
                         next_step(e, t)
                     else:
-                        last_step(t)
+                        last_step(t, direct=back == 1)
 
     mine = me // sharers
-    total = pow_v[mine]
-    with scope("waitpow"):
-        whole(pow_recv.at[: tiles - 1], pow_sem).wait()
-    for u in range(tiles):
-        total = total + jnp.where(u != mine, pow_recv[u], 0.0)
-    pow_mine[...] = total
+    straight = (tiles - 1 + ROTATE) % tiles if special else tiles
 
     def pair_copy(e):
         return pltpu.make_async_remote_copy(
@@ -500,12 +514,34 @@
             device_id_type=MESH,
         )
 
-    for e in range(1, sharers):
-        pair_copy(e).start()
-    for e in range(1, sharers):
-        with jax.named_scope("waitpair"):
-            pair_copy(e).wait_recv()
-        total = total + pow_pair[e - 1]
+    @pl.when(mine != straight)
+    def _():
+        with scope("waitpow"):
+            whole(pow_recv.at[: tiles - 1], pow_sems.at[0]).wait()
+        total = pow_v[mine]
+        for u in range(tiles):
+            total = total + jnp.where(u != mine, pow_recv[u], 0.0)
+        pow_mine[...] = total
+        for e in range(1, sharers):
+            pair_copy(e).start()
+        with scope("waitpair"):
+            for e in range(1, sharers):
+                pair_copy(e).wait_recv()
+                total = total + pow_pair[e - 1]
+        pow_total[...] = total
+
+    if special:
+
+        @pl.when(mine == straight)
+        def _():
+            with scope("waitpow"):
+                whole(pow_direct.at[: devices - 1], pow_sems.at[1]).wait()
+            total = pow_v[mine]
+            for d in range(devices):
+                total = total + jnp.where(d != me, pow_direct[d], 0.0)
+            pow_total[...] = total
+
+    total = pow_total[...]
     ell = mine * tile + lax.broadcasted_iota(jnp.int32, total.shape, 1)
     total = total / (2 * ell + 1).astype(F32)
     share = tile // sharers
@@ -520,9 +556,25 @@
         whole(coef_send, sent_sems.at[1]).wait()
         for s in range(steps):
             whole(halves[2 * s], sent_sems.at[2 + s]).wait()
-    for e in range(1, sharers):
-        pair_copy(e).wait_send()
-    whole(pow_v.at[: tiles - 1], sent_sems.at[2 + steps]).wait()
+    if special:
+
+        @pl.when(mine == straight)
+        def _():
+            whole(pow_v.at[: tiles - 1], sent_sems.at[2 + steps]).wait()
+            whole(pow_v.at[: sharers - 1], sent_sems.at[3 + steps]).wait()
+
+        @pl.when(mine != straight)
+        def _():
+            whole(pow_v.at[: tiles - 2], sent_sems.at[2 + steps]).wait()
+            whole(pow_v.at[:sharers], sent_sems.at[3 + steps]).wait()
+
+    else:
+        whole(pow_v.at[: tiles - 1], sent_sems.at[2 + steps]).wait()
+
+    @pl.when(mine != straight)
+    def _():
+        for e in range(1, sharers):
+            pair_copy(e).wait_send()
 
 
 def hand_over_body(large_ref, small_ref, large_out, small_out, sems):
@@ -593,14 +645,16 @@
         pltpu.VMEM((tiles, pairs, tile), F32),
         pltpu.VMEM((pairs, tile), F32),
         pltpu.VMEM((sharers - 1, pairs, tile), F32),
+        pltpu.VMEM((pairs, tile), F32),
+        pltpu.VMEM((devices, pairs, tile), F32),
         pltpu.SemaphoreType.DMA((4,)),
         pltpu.SemaphoreType.DMA,
         pltpu.SemaphoreType.DMA((5,)),
-        pltpu.SemaphoreType.DMA((3 + steps,)),
+        pltpu.SemaphoreType.DMA((4 + steps,)),
         pltpu.SemaphoreType.DMA((SLOTS, 2)),
         pltpu.SemaphoreType.DMA((2, 2)),
         pltpu.SemaphoreType.DMA((steps, SLOTS, 2)),
-        pltpu.SemaphoreType.DMA,
+        pltpu.SemaphoreType.DMA((2,)),
         pltpu.SemaphoreType.DMA((2, sharers - 1)),
     ]
     anywhere = pl.BlockSpec(memory_space=pl.ANY)

time: 74.9 us -> 73.9 us (0.987)
  Pallas kernels: 74.1 us -> 73 us
    pallas_call x1, Pallas kernels: 73.1 us -> 72 us  [per_device(): pl.pallas_call(functools.partial(kernel, cfg), out_shape=[pltpu.VMEM((own...]
where the time goes in v6:
time: 73.9 us; the launch traced here: 73.7 us
  Pallas kernels  73 us (99%)
    pallas_call x1, Pallas kernels, per_device(): pl.pallas_call(functools.partial(kernel, cfg), out_shape=[pltpu.VMEM((own...  72 us

profile of v6, /device:TPU:31, one launch (start us, length us, event | category | flops | bytes accessed | tf_op | source)
XLA Modules:
  0.0 73.7 jit_solution(12304965733630717060)
XLA Ops:
  0.6 72.0 %shard_map.77 = (f32[64,2,2048]{2,1,0:T(2,128)S(1)}, f32[10,64]{1,0:T(8,128)S(1)}) custom-call(s32[512]{0:T(512)} %owner_hbm.1, s32[1,512]{1,0:T(1,128)} %bitcast.3, f32[4,4,4096]{2,1,0:T(4,128)} %sky_hbm.1, f32[64,32]{1,0:T(8,128)} %constant.6.clone.first_hbm, bf16[256,1024]{1,0:T(8,128)(2,1)} %constant.7.clone.high_hbm, ...), custom_call_target="tpu_custom_call" | custom-call | flops 4294967296 | bytes 8388608 | tf_op jit(solution)/shard_map/pallas_call | solution.py:662
  72.7 1.0 %shard_map.78 = (f32[64,2,2048]{2,1,0:T(2,128)}, f32[10,64]{1,0:T(8,128)}) custom-call(f32[64,2,2048]{2,1,0:T(2,128)S(1)} %get-tuple-element.6.large_ref, f32[10,64]{1,0:T(8,128)S(1)} %get-tuple-element.7.small_ref), custom_call_target="tpu_custom_call" | custom-call | flops 262144 | bytes 2097152 | tf_op jit(solution)/shard_map/pallas_call | solution.py:592

commit v7 on v6

--- a/solution.py
+++ b/solution.py
@@ -274,12 +274,11 @@
     count = maps * cycles
     columns = 2 * orders
     stages = []
-    first = first_v[...]
+    pixels = jnp.concatenate([sky_v[b // cycles, b % cycles] for b in range(count)], axis=1)
+    stage = jnp.dot(first_v[...], pixels, precision=lax.Precision.HIGHEST, preferred_element_type=F32)
     for b in range(count):
-        stage = jnp.dot(
-            first, sky_v[b // cycles, b % cycles], precision=lax.Precision.HIGHEST, preferred_element_type=F32
-        )
-        stages.append(jnp.concatenate([stage[:coarse], stage[coarse:]], axis=1))
+        lanes = slice(b * tile, (b + 1) * tile)
+        stages.append(jnp.concatenate([stage[:coarse, lanes], stage[coarse:, lanes]], axis=1))
     left_high, left_low = split_bf16(jnp.concatenate(stages, axis=0))
     spectral = []
     span = orders // 2

time: 73.9 us -> 73.9 us (level)
  no operation moved by 1% of the time
where the time goes in v7:
time: 73.9 us; the launch traced here: 73.7 us
  Pallas kernels  73.1 us (99%)
    pallas_call x1, Pallas kernels, per_device(): pl.pallas_call(functools.partial(kernel, cfg), out_shape=[pltpu.VMEM((own...  72.1 us

profile of v7, /device:TPU:31, one launch (start us, length us, event | category | flops | bytes accessed | tf_op | source)
XLA Modules:
  0.0 73.7 jit_solution(4191454262043990420)
XLA Ops:
  0.6 72.1 %shard_map.77 = (f32[64,2,2048]{2,1,0:T(2,128)S(1)}, f32[10,64]{1,0:T(8,128)S(1)}) custom-call(s32[512]{0:T(512)} %owner_hbm.1, s32[1,512]{1,0:T(1,128)} %bitcast.3, f32[4,4,4096]{2,1,0:T(4,128)} %sky_hbm.1, f32[64,32]{1,0:T(8,128)} %constant.6.clone.first_hbm, bf16[256,1024]{1,0:T(8,128)(2,1)} %constant.7.clone.high_hbm, ...), custom_call_target="tpu_custom_call" | custom-call | flops 4294967296 | bytes 8388608 | tf_op jit(solution)/shard_map/pallas_call | solution.py:661
  72.7 1.0 %shard_map.78 = (f32[64,2,2048]{2,1,0:T(2,128)}, f32[10,64]{1,0:T(8,128)}) custom-call(f32[64,2,2048]{2,1,0:T(2,128)S(1)} %get-tuple-element.6.large_ref, f32[10,64]{1,0:T(8,128)S(1)} %get-tuple-element.7.small_ref), custom_call_target="tpu_custom_call" | custom-call | flops 262144 | bytes 2097152 | tf_op jit(solution)/shard_map/pallas_call | solution.py:591
